TPU v7x, 256 devices: a whole 4x4x8 slice. The times are simulated.
256 devices in a mesh: tables: 16 (over z_hi, y), cells: 16 (over z_lo, x, core).
Axes of the slice: x: 4, y: 4, z: 8 (z_hi: 4, z_lo: 2; z = z_hi * 2 + z_lo), core: 2. Of those that a mesh axis runs over, the one named last changes fastest.
Arguments:
- cells_in: bfloat16 [16, 512, 112, 192], P('tables', 'cells'), may hold values from -6 to 6
- train_count: int32 [16], P('tables'), may hold values from 128 to 384
- feat_count: int32 [16], P('tables'), may hold values from 28 to 112
- feat_qkv: bfloat16 [192, 576], replicated, may hold values from -2 to 2
- feat_proj: bfloat16 [192, 192], replicated, may hold values from -2 to 2
- row_qkv: bfloat16 [192, 576], replicated, may hold values from -2 to 2
- row_proj: bfloat16 [192, 192], replicated, may hold values from -0.4375 to 0.4375
- w_in: bfloat16 [192, 768], replicated, may hold values from -0.4375 to 0.4375
- w_out: bfloat16 [768, 192], replicated, may hold values from -0.21875 to 0.21875
- cotangent: bfloat16 [16, 512, 112, 192], P('tables', 'cells'), may hold values from -6 to 6
Outputs:
- cells_out: bfloat16 [16, 512, 112, 192], P('tables', 'cells')
- grad_in: float32 [192, 768], P(None, ('tables', 'cells'))
- grad_out: float32 [768, 192], P(('tables', 'cells'))
All inputs are finite; a program needn't handle non-finite values.
Results may differ from a plain program's by a relative error of at most 0.018.
Values may be sent and summed in bfloat16 or wider, within the bound.
A program may use at most 128 MiB of HBM per device.

v0:
```python
import math

import jax
import jax.numpy as jnp
from jax import lax
from jax.sharding import PartitionSpec as P

HEADS = 6
HEAD_DIM = 32


def split_up(x, dim, peers):
    before, after = (x.shape[:dim], x.shape[dim + 1 :])
    return jnp.moveaxis(x.reshape(*before, peers, -1, *after), dim, 0)


def sum_packed(arrays, axis, dims):
    peers = lax.axis_size(axis)
    pieces = [split_up(a, dim, peers) for a, dim in zip(arrays, dims)]
    lines = jnp.concatenate([b.reshape(peers, -1) for b in pieces], axis=1)
    rows = max(16, -(-lines.shape[1] // 1024) * 8)
    lines = jnp.pad(lines, ((0, 0), (0, rows * 128 - lines.shape[1]))).reshape(-1, 128)
    ravelled, at, gathered = (lax.psum_scatter(lines, axis, tiled=True).reshape(-1), 0, [])
    for b in pieces:
        part = b[0]
        gathered.append(ravelled[at : at + part.size].reshape(part.shape))
        at += part.size
    return tuple(gathered)


def sent_and_summed(x, axis, dim):
    peers = lax.axis_size(axis)
    pieces = lax.all_to_all(split_up(x, dim, peers), axis, 0, 0, tiled=True)
    return jnp.sum(pieces.astype(jnp.float32), axis=0)


def layer_norm(values):
    mean = jnp.mean(values, axis=-1, keepdims=True)
    centred = values - mean
    var = jnp.mean(centred * centred, axis=-1, keepdims=True)
    return centred / jnp.sqrt(var + 1e-05)


def feature_layer(block, feat_limit, weight_qkv, weight_proj):
    rows, feats, width = block.shape
    packed = jnp.dot(
        block.reshape(rows * feats, width), weight_qkv, preferred_element_type=jnp.float32
    )
    packed = packed.astype(jnp.bfloat16).reshape(rows, feats, 3, HEADS, HEAD_DIM)
    query, keys, values = (packed[:, :, 0], packed[:, :, 1], packed[:, :, 2])
    score = jnp.einsum(
        "rfhd,rghd->rhfg", query, keys, preferred_element_type=jnp.float32
    ) / jnp.sqrt(jnp.float32(HEAD_DIM))
    keep = jnp.arange(feats, dtype=jnp.int32) < feat_limit
    score = jnp.where(keep[None, None, None, :], score, jnp.float32(-1e30))
    probs = jax.nn.softmax(score, axis=-1).astype(jnp.bfloat16)
    attended = jnp.einsum(
        "rhfg,rghd->rfhd", probs, values, preferred_element_type=jnp.float32
    ).astype(jnp.bfloat16)
    mixed = jnp.dot(
        attended.reshape(rows * feats, width), weight_proj, preferred_element_type=jnp.float32
    )
    total = block.reshape(rows * feats, width).astype(jnp.float32) + mixed
    return layer_norm(total).astype(jnp.bfloat16).reshape(rows, feats, width)


def row_single(column, train_limit, weight_qkv, weight_proj):
    rows, width = column.shape
    packed = jnp.dot(column, weight_qkv, preferred_element_type=jnp.float32)
    packed = packed.astype(jnp.bfloat16).reshape(rows, 3, HEADS, HEAD_DIM)
    query, keys, values = (packed[:, 0], packed[:, 1], packed[:, 2])
    score = jnp.einsum("ihd,jhd->hij", query, keys, preferred_element_type=jnp.float32) / jnp.sqrt(
        jnp.float32(HEAD_DIM)
    )
    keep = jnp.arange(rows, dtype=jnp.int32) < train_limit
    score = jnp.where(keep[None, None, :], score, jnp.float32(-1e30))
    probs = jax.nn.softmax(score, axis=-1).astype(jnp.bfloat16)
    attended = jnp.einsum("hij,jhd->ihd", probs, values, preferred_element_type=jnp.float32)
    attended = attended.astype(jnp.bfloat16).reshape(rows, width)
    mixed = jnp.dot(attended, weight_proj, preferred_element_type=jnp.float32)
    return layer_norm(column.astype(jnp.float32) + mixed).astype(jnp.bfloat16)


def exact_gelu(values):
    return jax.nn.gelu(values, approximate=False)


def dense_block(normed_cells, cot_cells, w_in, w_out):
    shape = normed_cells.shape
    normed = normed_cells.reshape(-1, shape[-1])
    cot_flat = cot_cells.reshape(-1, shape[-1])
    pre = jnp.dot(normed, w_in, preferred_element_type=jnp.float32)
    act_f, backward = jax.vjp(exact_gelu, pre)
    act = act_f.astype(jnp.bfloat16)
    output = (
        normed.astype(jnp.float32) + jnp.dot(act, w_out, preferred_element_type=jnp.float32)
    ).astype(jnp.bfloat16)
    contract = (((0,), (0,)), ((), ()))
    part_out = lax.dot_general(act, cot_flat, contract, preferred_element_type=jnp.float32)
    dact = lax.dot_general(
        cot_flat, w_out, (((1,), (1,)), ((), ())), preferred_element_type=jnp.float32
    )
    dpre = backward(dact)[0].astype(jnp.bfloat16)
    part_in = lax.dot_general(normed, dpre, contract, preferred_element_type=jnp.float32)
    return (output.reshape(shape), part_in, part_out)


def per_device(
    cells_in,
    train_count,
    feat_count,
    feat_qkv,
    feat_proj,
    row_qkv,
    row_proj,
    w_in,
    w_out,
    cotangent,
):
    block = cells_in[0]
    train_limit = train_count[0]
    feat_limit = feat_count[0]
    groups = lax.axis_size("cells")
    mid = feature_layer(block, feat_limit, feat_qkv, feat_proj)
    local_rows, feats, width = mid.shape
    grouped = mid.reshape(local_rows, groups, feats // groups, width)
    columns = jnp.moveaxis(
        lax.all_to_all(grouped, "cells", split_axis=1, concat_axis=0, tiled=True)[:, 0], 1, 0
    )
    done = lax.map(lambda column: row_single(column, train_limit, row_qkv, row_proj), columns)
    exchanged = jnp.moveaxis(done, 0, 1)[:, None]
    normed_cols = exchanged.reshape(local_rows * groups, feats // groups, width)
    normed = lax.all_to_all(normed_cols, "cells", split_axis=0, concat_axis=1, tiled=True)
    output, part_in, part_out = dense_block(normed, cotangent[0], w_in, w_out)
    whole_rows = block.shape[0] * groups
    factor = 1.0 / math.sqrt(lax.axis_size("tables") * whole_rows * block.shape[1])
    part_in = part_in * factor
    part_out = part_out * factor
    table_in, table_out = tuple(
        (
            part.astype(jnp.float32)
            for part in sum_packed(
                (part_in.astype(jnp.bfloat16), part_out.astype(jnp.bfloat16)), "tables", (1, 0)
            )
        )
    )
    grad_in, grad_out = (
        sent_and_summed(table_in.astype(jnp.bfloat16), "cells", 1),
        sent_and_summed(table_out.astype(jnp.bfloat16), "cells", 0),
    )
    return (output[None], grad_in, grad_out)


def solution(mesh):
    return jax.shard_map(
        per_device,
        mesh=mesh,
        in_specs=(
            P("tables", "cells", None, None),
            P("tables"),
            P("tables"),
            P(),
            P(),
            P(),
            P(),
            P(),
            P(),
            P("tables", "cells", None, None),
        ),
        out_specs=(
            P("tables", "cells", None, None),
            P(None, ("tables", "cells")),
            P(("tables", "cells"), None),
        ),
        check_vma=False,
    )
```

profile of v0, /device:TPU:1, one launch (start us, length us, event | category | flops | bytes accessed | tf_op | source)
XLA Modules:
  0.0 405.7 jit_solution(5185605129910732992)
XLA Ops:
  7.2 2.5 copy.64
  9.7 3.1 reshape_squeeze.7
  12.8 4.2 %convolution_convert_fusion.1 = bf16[3584,576]{0,1:T(8,128)(2,1)} fusion(bf16[3584,192]{0,1:T(8,128)(2,1)S(1)} %reshape_squeeze.7, bf16[192,576]{1,0:T(8,128)(2,1)} %param.15), kind=kOutput, calls=%fused_computation.50 | convolution fusion | flops 794787840 | bytes 5726208 | tf_op jit(solution)/shard_map/dot_general | solution.py:46
  17.0 9.7 %reshape.83 = bf16[32,112,3,6,32]{1,0,4,3,2:T(8,128)(2,1)} reshape(bf16[3584,576]{0,1:T(8,128)(2,1)} %convolution_convert_fusion.1) | data formatting | bytes 8257536 | tf_op jit(solution)/shard_map/reshape | solution.py:49
  26.7 3.2 fusion.43
  30.5 6.8 %fusion.30 = f32[32,6,112,112]{2,3,1,0:T(8,128)} fusion(bf16[32,112,1,6,32]{1,0,4,3,2:T(8,128)(2,1)S(1)} %get-tuple-element.86, bf16[32,112,1,6,32]{1,0,4,3,2:T(8,128)(2,1)S(1)} %get-tuple-element.85), kind=kOutput, calls=%fused_computation.63 | convolution fusion | flops 154140672 | bytes 12386304 | tf_op jit(solution)/shard_map/rfhd,rghd->rhfg/dot_general | solution.py:51
  37.4 15.7 %fusion.45 = (f32[32,6,112]{2,1,0:T(8,128)S(1)}, f32[32,6,112,112]{2,3,1,0:T(8,128)}) fusion(f32[32,6,112,112]{2,3,1,0:T(8,128)} %fusion.30, pred[112]{0:T(512)(128)(4,1)S(1)} %iota_compare_fusion.1), kind=kOutput, calls=%fused_computation.86 | output fusion | flops 14450799 | bytes 19353712 | tf_op jit(solution)/shard_map/sub | solution.py:56
  53.1 6.6 %fusion.31 = bf16[32,112,6,32]{1,3,2,0:T(8,128)(2,1)S(1)} fusion(f32[32,6,112,112]{2,3,1,0:T(8,128)} %get-tuple-element.90, f32[32,6,112]{2,1,0:T(8,128)S(1)} %get-tuple-element.89, bf16[32,112,1,6,32]{1,0,4,3,2:T(8,128)(2,1)S(1)} %get-tuple-element.84), kind=kOutput, calls=%fused_computation.66 | convolution fusion | flops 159645696 | bytes 12472320 | tf_op jit(solution)/shard_map/rhfg,rghd->rfhd/dot_general | solution.py:57
  59.7 1.0 copy.69
  60.7 4.0 reshape.84
  64.7 1.9 fusion.46
  67.3 2.3 copy.70
  69.6 3.0 reshape_reshape.6
  72.6 2.4 copy.71
  75.0 7.2 %all-to-all-start = ((bf16[32,16,7,192]{3,0,2,1:T(8,128)(2,1)}), bf16[32,16,7,192]{3,0,2,1:T(8,128)(2,1)S(1)}, u32[]{:S(2)}, u32[]{:S(2)}) async-start(bf16[32,16,7,192]{3,0,2,1:T(8,128)(2,1)} %copy.71), calls=%async_computation | async-start | bytes 3670016 | tf_op jit(solution)/shard_map/all_to_all | solution.py:128
  82.2 24.5 %all-to-all-done = bf16[32,16,7,192]{3,0,2,1:T(8,128)(2,1)S(1)} async-done(((bf16[32,16,7,192]{3,0,2,1:T(8,128)(2,1)}), bf16[32,16,7,192]{3,0,2,1:T(8,128)(2,1)S(1)}, u32[]{:S(2)}, u32[]{:S(2)}) %all-to-all-start) | async-done | bytes 1376288 | tf_op jit(solution)/shard_map/all_to_all | solution.py:128
  106.7 1.4 copy.72
  108.1 2.9 copy.73
  111.0 74.9 %while.10 = (s32[]{:T(128)}, bf16[7,512,192]{1,2,0:T(8,128)(2,1)}, bf16[7,512,192]{1,2,0:T(8,128)(2,1)S(1)}, bf16[192,576]{1,0:T(8,128)(2,1)S(1)}, s32[]{:T(128)}, /*index=5*/bf16[192,192]{1,0:T(8,128)(2,1)S(1)}, s32[]{:T(128)}) while((s32[]{:T(128)}, bf16[7,512,192]{1,2,0:T(8,128)(2,1)}, bf16[7,512,192]{1,2,0:T(8,128)(2,1)S(1)}, ...), condition=%wide.region_9.10_spmd, body=%wide.region_4.9_spmd.sunk | while | flops 363038208 | bytes 16293465 | solution.py:130
  112.0 5.1 %fusion.74 = (f32[6,512]{1,0:T(8,128)S(1)}, f32[6,512,512]{1,2,0:T(8,128)}) fusion(pred[512]{0:T(512)(128)(4,1)S(1)} %iota_compare_fusion.3, bf16[512,3,6,32]{0,3,2,1:T(8,128)(2,1)S(1)} %bitcast.117), kind=kOutput, calls=%fused_computation.82.clone.1 | convolution fusion | flops 106955264 | bytes 6697472 | tf_op jit(solution)/shard_map/while/body/eval_jaxpr/sub | solution.py:77
  117.1 3.4 fusion.75
  121.0 0.7 bitcast_dynamic-update-slice_fusion.2
  122.7 5.1 %fusion.74 = (f32[6,512]{1,0:T(8,128)S(1)}, f32[6,512,512]{1,2,0:T(8,128)}) fusion(pred[512]{0:T(512)(128)(4,1)S(1)} %iota_compare_fusion.3, bf16[512,3,6,32]{0,3,2,1:T(8,128)(2,1)S(1)} %bitcast.117), kind=kOutput, calls=%fused_computation.82.clone.1 | convolution fusion | flops 106955264 | bytes 6697472 | tf_op jit(solution)/shard_map/while/body/eval_jaxpr/sub | solution.py:77
  127.8 3.4 fusion.75
  131.7 0.7 bitcast_dynamic-update-slice_fusion.2
  133.4 5.1 %fusion.74 = (f32[6,512]{1,0:T(8,128)S(1)}, f32[6,512,512]{1,2,0:T(8,128)}) fusion(pred[512]{0:T(512)(128)(4,1)S(1)} %iota_compare_fusion.3, bf16[512,3,6,32]{0,3,2,1:T(8,128)(2,1)S(1)} %bitcast.117), kind=kOutput, calls=%fused_computation.82.clone.1 | convolution fusion | flops 106955264 | bytes 6697472 | tf_op jit(solution)/shard_map/while/body/eval_jaxpr/sub | solution.py:77
  138.5 3.4 fusion.75
  142.3 0.7 bitcast_dynamic-update-slice_fusion.2
  144.1 5.1 %fusion.74 = (f32[6,512]{1,0:T(8,128)S(1)}, f32[6,512,512]{1,2,0:T(8,128)}) fusion(pred[512]{0:T(512)(128)(4,1)S(1)} %iota_compare_fusion.3, bf16[512,3,6,32]{0,3,2,1:T(8,128)(2,1)S(1)} %bitcast.117), kind=kOutput, calls=%fused_computation.82.clone.1 | convolution fusion | flops 106955264 | bytes 6697472 | tf_op jit(solution)/shard_map/while/body/eval_jaxpr/sub | solution.py:77
  149.2 3.4 fusion.75
  153.0 0.7 bitcast_dynamic-update-slice_fusion.2
  154.8 5.1 %fusion.74 = (f32[6,512]{1,0:T(8,128)S(1)}, f32[6,512,512]{1,2,0:T(8,128)}) fusion(pred[512]{0:T(512)(128)(4,1)S(1)} %iota_compare_fusion.3, bf16[512,3,6,32]{0,3,2,1:T(8,128)(2,1)S(1)} %bitcast.117), kind=kOutput, calls=%fused_computation.82.clone.1 | convolution fusion | flops 106955264 | bytes 6697472 | tf_op jit(solution)/shard_map/while/body/eval_jaxpr/sub | solution.py:77
  159.9 3.4 fusion.75
  163.7 0.7 bitcast_dynamic-update-slice_fusion.2
  165.5 5.1 %fusion.74 = (f32[6,512]{1,0:T(8,128)S(1)}, f32[6,512,512]{1,2,0:T(8,128)}) fusion(pred[512]{0:T(512)(128)(4,1)S(1)} %iota_compare_fusion.3, bf16[512,3,6,32]{0,3,2,1:T(8,128)(2,1)S(1)} %bitcast.117), kind=kOutput, calls=%fused_computation.82.clone.1 | convolution fusion | flops 106955264 | bytes 6697472 | tf_op jit(solution)/shard_map/while/body/eval_jaxpr/sub | solution.py:77
  170.6 3.4 fusion.75
  174.4 0.7 bitcast_dynamic-update-slice_fusion.2
  176.2 5.1 %fusion.74 = (f32[6,512]{1,0:T(8,128)S(1)}, f32[6,512,512]{1,2,0:T(8,128)}) fusion(pred[512]{0:T(512)(128)(4,1)S(1)} %iota_compare_fusion.3, bf16[512,3,6,32]{0,3,2,1:T(8,128)(2,1)S(1)} %bitcast.117), kind=kOutput, calls=%fused_computation.82.clone.1 | convolution fusion | flops 106955264 | bytes 6697472 | tf_op jit(solution)/shard_map/while/body/eval_jaxpr/sub | solution.py:77
  181.3 3.4 fusion.75
  185.1 0.7 bitcast_dynamic-update-slice_fusion.2
  185.9 4.4 %copy.74 = bf16[7,512,192]{2,0,1:T(8,128)(2,1)} copy(bf16[7,512,192]{1,2,0:T(8,128)(2,1)} %get-tuple-element.35) | data formatting | bytes 2752512 | tf_op jit(solution)/shard_map/while | solution.py:130
  190.2 5.5 %all-to-all-start.1 = ((bf16[512,7,192]{2,1,0:T(8,128)(2,1)}), bf16[512,7,192]{2,1,0:T(8,128)(2,1)S(1)}, u32[]{:S(2)}, u32[]{:S(2)}) async-start(bf16[512,7,192]{2,1,0:T(8,128)(2,1)} %bitcast.120), calls=%async_computation.1 | async-start | bytes 4194304 | tf_op jit(solution)/shard_map/all_to_all | solution.py:133
  195.7 3.6 copy.78
  199.3 4.4 %reshape_squeeze.8 = bf16[3584,192]{0,1:T(8,128)(2,1)} reshape(bf16[1,32,112,192]{2,1,3,0:T(8,128)(2,1)} %copy.78) | data formatting | bytes 2752512 | tf_op jit(solution)/shard_map/reshape;squeeze | solution.py:91
  203.7 19.6 %all-to-all-done.1 = bf16[512,7,192]{2,1,0:T(8,128)(2,1)S(1)} async-done(((bf16[512,7,192]{2,1,0:T(8,128)(2,1)}), bf16[512,7,192]{2,1,0:T(8,128)(2,1)S(1)}, u32[]{:S(2)}, u32[]{:S(2)}) %all-to-all-start.1) | async-done | bytes 1376288 | tf_op jit(solution)/shard_map/all_to_all | solution.py:133
  223.3 1.6 copy.76
  224.9 2.9 reshape.85
  227.8 27.8 %multiply_convert_fusion = (bf16[3584,768]{1,0:T(8,128)(2,1)}, f32[3584,768]{1,0:T(8,128)}, f32[3584,768]{1,0:T(8,128)}) fusion(bf16[3584,192]{1,0:T(8,128)(2,1)S(1)} %reshape.85, bf16[192,768]{1,0:T(8,128)(2,1)S(1)} %copy-done), kind=kOutput, calls=%fused_computation.32 | convolution fusion | flops 1235877888 | bytes 29196288 | tf_op jit(solution)/shard_map/dot_general | solution.py:92
  255.6 13.1 %fusion.34 = bf16[192,768]{1,0:T(8,128)(2,1)S(1)} fusion(bf16[3584,192]{1,0:T(8,128)(2,1)S(1)} %reshape.85, f32[3584,768]{1,0:T(8,128)} %get-tuple-element.79, f32[3584,768]{1,0:T(8,128)} %get-tuple-element.93, bf16[3584,192]{0,1:T(8,128)(2,1)S(1)} %copy-done.4, bf16[768,192]{0,1:T(8,128)(2,1)} %param.20), kind=kOutput, calls=%fused_computation.70 | convolution fusion | flops 2152759296 | bytes 25362432 | tf_op jit(solution)/shard_map/dot_general | solution.py:104
  269.3 1.4 reshape.87
  270.7 4.2 %fusion.33 = bf16[768,192]{0,1:T(8,128)(2,1)S(1)} fusion(bf16[3584,192]{0,1:T(8,128)(2,1)} %reshape_squeeze.8, bf16[3584,768]{1,0:T(8,128)(2,1)} %get-tuple-element.78), kind=kOutput, calls=%fused_computation.69 | convolution fusion | flops 1057259520 | bytes 7176192 | tf_op jit(solution)/shard_map/dot_general | solution.py:99
  275.5 1.1 reshape.88
  276.6 1.4 copy.77
  278.0 86.2 %reduce-scatter.2.cloned.1.call-done = bf16[144,128]{1,0:T(8,128)(2,1)} async-done(((bf16[2304,128]{1,0:T(8,128)(2,1)}), bf16[144,128]{1,0:T(8,128)(2,1)}) %reduce-scatter.2.cloned.1.call-update) | async-done | bytes 36880 | tf_op jit(solution)/shard_map/reduce_scatter | solution.py:23
  364.2 0.7 fusion.44
  365.0 1.6 reshape.89
  366.5 1.3 copy.82
  367.9 7.2 %all-to-all-start.2 = ((bf16[16,192,3]{1,2,0:T(4,128)(2,1)}), bf16[16,192,3]{1,2,0:T(4,128)(2,1)S(1)}, u32[]{:S(2)}, u32[]{:S(2)}) async-start(bf16[16,192,3]{1,2,0:T(4,128)(2,1)} %copy.82), calls=%async_computation.3 | async-start | bytes 65536 | tf_op jit(solution)/shard_map/all_to_all | solution.py:33
  375.1 5.6 %fusion.27 = bf16[3584,192]{0,1:T(8,128)(2,1)} fusion(bf16[3584,768]{1,0:T(8,128)(2,1)} %get-tuple-element.78, bf16[768,192]{0,1:T(8,128)(2,1)} %param.20, bf16[3584,192]{0,1:T(8,128)(2,1)S(1)} %copy.77), kind=kOutput, calls=%fused_computation.57 | convolution fusion | flops 1059028992 | bytes 8552448 | tf_op jit(solution)/shard_map/dot_general | solution.py:96
  380.7 3.4 broadcast_in_dim_reshape.3
  384.1 1.8 copy.85
  385.8 0.7 reshape.90
  386.5 5.7 %all-to-all-start.3 = ((bf16[16,3,192]{2,1,0:T(4,128)(2,1)}), bf16[16,3,192]{2,1,0:T(4,128)(2,1)S(1)}, u32[]{:S(2)}, u32[]{:S(2)}) async-start(bf16[16,3,192]{2,1,0:T(4,128)(2,1)} %reshape.90), calls=%async_computation.4 | async-start | bytes 65536 | tf_op jit(solution)/shard_map/all_to_all | solution.py:33
  392.8 5.2 %all-to-all-done.3 = bf16[16,3,192]{2,1,0:T(4,128)(2,1)S(1)} async-done(((bf16[16,3,192]{2,1,0:T(4,128)(2,1)}), bf16[16,3,192]{2,1,0:T(4,128)(2,1)S(1)}, u32[]{:S(2)}, u32[]{:S(2)}) %all-to-all-start.3) | async-done | bytes 18464 | tf_op jit(solution)/shard_map/all_to_all | solution.py:33
  (70 shorter events, 12.7 us)
Async XLA Ops:
  7.2 220.6 %copy-start = (bf16[192,768]{1,0:T(8,128)(2,1)S(1)}, bf16[192,768]{1,0:T(8,128)(2,1)}, u32[]{:S(2)}) copy-start(bf16[192,768]{1,0:T(8,128)(2,1)} %param.19) | copy-start | bytes 884740
  53.1 11.6 %copy-start.5 = (bf16[192,192]{1,0:T(8,128)(2,1)S(1)}, bf16[192,192]{1,0:T(8,128)(2,1)}, u32[]{:S(2)}) copy-start(bf16[192,192]{1,0:T(8,128)(2,1)} %param.16) | copy-start | bytes 221188
  67.2 43.7 %copy-start.2 = (bf16[192,576]{1,0:T(8,128)(2,1)S(1)}, bf16[192,576]{1,0:T(8,128)(2,1)}, u32[]{:S(2)}) copy-start(bf16[192,576]{1,0:T(8,128)(2,1)} %param.17) | copy-start | bytes 663556
  67.2 43.7 %copy-start.3 = (bf16[192,192]{1,0:T(8,128)(2,1)S(1)}, bf16[192,192]{1,0:T(8,128)(2,1)}, u32[]{:S(2)}) copy-start(bf16[192,192]{1,0:T(8,128)(2,1)} %param.18) | copy-start | bytes 221188
  75.0 31.6 %all-to-all-start = ((bf16[32,16,7,192]{3,0,2,1:T(8,128)(2,1)}), bf16[32,16,7,192]{3,0,2,1:T(8,128)(2,1)S(1)}, u32[]{:S(2)}, u32[]{:S(2)}) async-start(bf16[32,16,7,192]{3,0,2,1:T(8,128)(2,1)} %copy.71), calls=%async_computation | async-start | bytes 3670016 | tf_op jit(solution)/shard_map/all_to_all | solution.py:128
  190.2 33.1 %all-to-all-start.1 = ((bf16[512,7,192]{2,1,0:T(8,128)(2,1)}), bf16[512,7,192]{2,1,0:T(8,128)(2,1)S(1)}, u32[]{:S(2)}, u32[]{:S(2)}) async-start(bf16[512,7,192]{2,1,0:T(8,128)(2,1)} %bitcast.120), calls=%async_computation.1 | async-start | bytes 4194304 | tf_op jit(solution)/shard_map/all_to_all | solution.py:133
  195.7 168.5 %reduce-scatter.2.cloned.1.call-start = ((), (), s32[]{:S(2)}) async-start(), calls=%async_computation.5 | async-start | bytes 626688 | tf_op jit(solution)/shard_map/reduce_scatter | solution.py:23
  227.8 27.8 %copy-start.4 = (bf16[3584,192]{0,1:T(8,128)(2,1)S(1)}, bf16[3584,192]{0,1:T(8,128)(2,1)}, u32[]{:S(2)}) copy-start(bf16[3584,192]{0,1:T(8,128)(2,1)} %reshape_squeeze.8) | copy-start | bytes 4128772
  276.6 122.0 %copy-start.1 = (bf16[192,768]{1,0:T(8,128)(2,1)S(1)}, bf16[192,768]{1,0:T(8,128)(2,1)}, u32[]{:S(2)}) copy-start(bf16[192,768]{1,0:T(8,128)(2,1)} %param.19) | copy-start | bytes 884740
  367.9 18.7 %all-to-all-start.2 = ((bf16[16,192,3]{1,2,0:T(4,128)(2,1)}), bf16[16,192,3]{1,2,0:T(4,128)(2,1)S(1)}, u32[]{:S(2)}, u32[]{:S(2)}) async-start(bf16[16,192,3]{1,2,0:T(4,128)(2,1)} %copy.82), calls=%async_computation.3 | async-start | bytes 65536 | tf_op jit(solution)/shard_map/all_to_all | solution.py:33
  386.5 11.5 %all-to-all-start.3 = ((bf16[16,3,192]{2,1,0:T(4,128)(2,1)}), bf16[16,3,192]{2,1,0:T(4,128)(2,1)S(1)}, u32[]{:S(2)}, u32[]{:S(2)}) async-start(bf16[16,3,192]{2,1,0:T(4,128)(2,1)} %reshape.90), calls=%async_computation.4 | async-start | bytes 65536 | tf_op jit(solution)/shard_map/all_to_all | solution.py:33
Sparse Core Ops, SparseCore 0:
  276.7 87.4 reduce-scatter.1
where the time goes:
time: 413 us; the launch traced here: 406 us
  matrix products  135 us (33%)
  waiting for transfers between devices  135 us (33%)
  local copies, waits for them, and re-layouts  66.8 us (16%)
  other arithmetic  27.8 us (7%)
  starting transfers between devices  25.6 us (6%)
  between operations  15.1 us (4%)
    reduce_scatter x1, waiting for transfers between devices, sum_packed(): lax.psum_scatter(lines, axis, tiled=True).reshape(-1)  86.2 us
    sub x7, matrix products, row_single(): probs = jax.nn.softmax(score, axis=-1).astype(jnp.bfloat16)  35.9 us
    dot_general x1, matrix products, dense_block(): pre = jnp.dot(normed, w_in, preferred_element_type=jnp.float32)  27.8 us
    all_to_all x1, waiting for transfers between devices, per_device(): lax.all_to_all(grouped, 'cells', split_axis=1, concat_axis=0, tiled=True)  24.5 us
    dot_general x7, matrix products, row_single(): jnp.einsum('hij,jhd->ihd', probs, values, preferred_element_type=jnp.floa...  24.1 us
    all_to_all x1, waiting for transfers between devices, per_device(): lax.all_to_all(normed_cols, 'cells', split_axis=0, concat_axis=1, tiled=T...  19.6 us
    sub x1, other arithmetic, feature_layer(): probs = jax.nn.softmax(score, axis=-1).astype(jnp.bfloat16)  15.7 us
    dot_general x1, matrix products, dense_block(): lax.dot_general(normed, dpre, contract, preferred_element_type=jnp.float32)  13.1 us
  transfers between devices with their start and end apart: 5, of which 4 were waited for; matrix products, arithmetic and copies ran while one was open for 5% of the time, Pallas kernels for 0%

commit v1 on v0

v1 whole, which is shorter than its diff:
```python
import functools
import math

import jax
import jax.numpy as jnp
from jax import lax
from jax.experimental import pallas as pl
from jax.experimental.pallas import tpu as pltpu
from jax.sharding import PartitionSpec as P

HEADS = 6
HEAD_DIM = 32
E = 192
HID = 768
FEATS = 112
ROWS = 512
LOCAL = 32
PEERS = 16
OWN = 7
KEYS = 384
STRIDE = 40
F32 = jnp.float32
BF16 = jnp.bfloat16
NEG = -1e30
QSCALE = math.log2(math.e) / math.sqrt(HEAD_DIM)
VMEM_LIMIT = 60 * 1024 * 1024
MESH = pl.DeviceIdType.MESH

NN = (((1,), (0,)), ((), ()))
NT = (((1,), (1,)), ((), ()))


def mm(a, b, dims=NN):
    return lax.dot_general(a, b, dims, preferred_element_type=F32)


def eye(n):
    r = lax.broadcasted_iota(jnp.int32, (n, n), 0)
    c = lax.broadcasted_iota(jnp.int32, (n, n), 1)
    return (r == c).astype(F32).astype(BF16)


def head_mask(head):
    lane = lax.broadcasted_iota(jnp.int32, (1, 128), 1)
    low = 32 * (head % 4)
    return ((lane >= low) & (lane < low + 32)).astype(F32).astype(BF16)


def ones_mask(head):
    lane = lax.broadcasted_iota(jnp.int32, (1, 128), 1)
    low = 32 * (head % 4)
    high = 128 if head == 5 else low + 32
    return ((lane >= low) & (lane < high)).astype(F32).astype(BF16)


def spread_weights(w_ref, wide_ref, proj_ref, proj_wide):
    wide_ref[...] = jnp.zeros(wide_ref.shape, BF16)
    for part in range(3):
        wide_ref[:, 256 * part : 256 * part + 192] = w_ref[:, 192 * part : 192 * part + 192]
    proj_wide[...] = jnp.zeros(proj_wide.shape, BF16)
    proj_wide[0:192, :] = proj_ref[...]


def layer_norm(total):
    mean = jnp.sum(total, axis=-1, keepdims=True) * (1.0 / E)
    centred = total - mean
    var = jnp.sum(centred * centred, axis=-1, keepdims=True) * (1.0 / E)
    return centred * lax.rsqrt(var + 1e-05)


def enter(axes):
    barrier = pltpu.get_barrier_semaphore()
    for axis in axes:
        me = lax.axis_index(axis)

        @pl.loop(1, PEERS)
        def _(k):
            pl.semaphore_signal(
                barrier, inc=1, device_id={axis: lax.rem(me + k, PEERS)}, device_id_type=MESH
            )

    pl.semaphore_wait(barrier, (PEERS - 1) * len(axes))


FBLOCK = 4


def feature_kernel(
    remote,
    count_ref,
    x_ref,
    w_ref,
    proj_ref,
    out_ref,
    wide,
    proj_wide,
    tok,
    qkv,
    vals0,
    vals1,
    att,
    turn0,
    turn1,
    send,
    send_sem,
    recv_sem,
):
    me = lax.axis_index("cells") if remote else 0
    if remote:
        enter(("cells",))
    spread_weights(w_ref, wide, proj_ref, proj_wide)
    ident = eye(FEATS)
    lane = lax.broadcasted_iota(jnp.int32, (1, 128), 1)
    bias = jnp.where(lane < count_ref[0], 0.0, NEG).astype(F32)
    for ref, heads in ((vals0, range(4)), (vals1, range(4, 6))):
        ref[...] = jnp.zeros(ref.shape, BF16)
        for j in range(FBLOCK):
            for i, h in enumerate(heads):
                ref[j, 128 * i : 128 * i + FEATS, 128:256] = jnp.broadcast_to(ones_mask(h), (FEATS, 128))
    zero_pad = jnp.zeros((128 - FEATS, 128), BF16)

    def block(step, _):
        for j in range(FBLOCK):
            tok[pl.ds(FEATS * j, FEATS), :] = mm(ident, x_ref[step * FBLOCK + j], NT)
        qkv[...] = mm(tok[...].astype(BF16), wide[...])
        for j in range(FBLOCK):
            rows = pl.ds(FEATS * j, FEATS)
            for tile, heads, vals in ((0, range(4), vals0), (1, range(4, 6), vals1)):
                at = 128 * tile
                q = (qkv[rows, at : at + 128] * QSCALE).astype(BF16)
                k = qkv[rows, 256 + at : 384 + at].astype(BF16)
                v = qkv[rows, 512 + at : 640 + at].astype(BF16)
                pieces = []
                for i, h in enumerate(heads):
                    pieces += [k * head_mask(h), zero_pad]
                    vals[j, 128 * i : 128 * i + FEATS, 0:128] = v * head_mask(h)
                score = mm(q, jnp.concatenate(pieces, axis=0), NT)
                probs = []
                for i, h in enumerate(heads):
                    s = score[:, 128 * i : 128 * i + 128] + bias
                    probs.append(jnp.exp2(s - jnp.max(s, axis=-1, keepdims=True)).astype(BF16))
                got = mm(jnp.concatenate(probs, axis=1), vals[j])
                att[rows, at : at + 128] = (got[:, :128] / got[:, 128:]).astype(BF16)
        total = tok[...] + mm(att[...], proj_wide[...])
        mid = layer_norm(total)
        for j in range(FBLOCK):
            at = step * FBLOCK + j
            turn0[pl.ds(at, FEATS, stride=STRIDE), :] = mid[FEATS * j : FEATS * j + FEATS, 0:128]
            turn1[pl.ds(at, FEATS, stride=STRIDE), 0:64] = mid[FEATS * j : FEATS * j + FEATS, 128:192]
        return 0

    def half(c, _):
        lax.fori_loop(c * (16 // FBLOCK), (c + 1) * (16 // FBLOCK), block, 0)
        base = pl.multiple_of(c * 16, 16)

        def to_peer(k, _):
            p = lax.rem(me + k, PEERS)
            for f in range(OWN):
                src = pl.multiple_of((p * OWN + f) * STRIDE + base, 8)
                send[p, f, pl.ds(base, 16), 0:128] = turn0[pl.ds(src, 16), :].astype(BF16)
                send[p, f, pl.ds(base, 16), 128:192] = turn1[pl.ds(src, 16), 0:64].astype(BF16)
            source = send.at[p, :, pl.ds(base, 16), :]
            target = out_ref.at[:, pl.ds(pl.multiple_of(me * LOCAL + base, 16), 16), :]

            if remote:

                @pl.when(k == 0)
                def _():
                    pltpu.make_async_copy(source, target, recv_sem).start()

                @pl.when(k != 0)
                def _():
                    pltpu.make_async_remote_copy(
                        src_ref=source,
                        dst_ref=target,
                        send_sem=send_sem,
                        recv_sem=recv_sem,
                        device_id={"cells": p},
                        device_id_type=MESH,
                    ).start()

            else:
                target = out_ref.at[:, pl.ds(pl.multiple_of(p * LOCAL + base, 16), 16), :]
                pltpu.make_async_copy(source, target, recv_sem).start()
            return 0

        return lax.fori_loop(0, PEERS, to_peer, 0)

    lax.fori_loop(0, 2, half, 0)
    pltpu.make_async_copy(out_ref, out_ref, recv_sem).wait()
    if remote:
        sent = send.at[pl.ds(0, PEERS - 1)]
        pltpu.make_async_copy(sent, sent, send_sem).wait()


def feature_layer(x_t, count, weight_qkv, weight_proj, remote=True):
    vmem = pl.BlockSpec(memory_space=pltpu.VMEM)
    return pl.pallas_call(
        functools.partial(feature_kernel, remote),
        name="feature_attention",
        out_shape=jax.ShapeDtypeStruct((OWN, ROWS, E), BF16),
        in_specs=[pl.BlockSpec(memory_space=pltpu.SMEM), vmem, vmem, vmem],
        out_specs=pl.BlockSpec(memory_space=pl.ANY),
        scratch_shapes=[
            pltpu.VMEM((E, 768), BF16),
            pltpu.VMEM((256, E), BF16),
            pltpu.VMEM((FBLOCK * FEATS, E), F32),
            pltpu.VMEM((FBLOCK * FEATS, 768), F32),
            pltpu.VMEM((FBLOCK, 512, 256), BF16),
            pltpu.VMEM((FBLOCK, 256, 256), BF16),
            pltpu.VMEM((FBLOCK * FEATS, 256), BF16),
            pltpu.VMEM((FEATS * STRIDE, 128), F32),
            pltpu.VMEM((FEATS * STRIDE, 128), F32),
            pltpu.VMEM((PEERS, OWN, LOCAL, E), BF16),
            pltpu.SemaphoreType.DMA,
            pltpu.SemaphoreType.DMA,
        ],
        compiler_params=pltpu.CompilerParams(
            collective_id=0 if remote else None, has_side_effects=True, vmem_limit_bytes=VMEM_LIMIT
        ),
    )(count, x_t, weight_qkv, weight_proj)


def row_kernel(
    remote,
    count_ref,
    x_ref,
    w_ref,
    proj_ref,
    out_ref,
    wide,
    proj_wide,
    qkv,
    keys,
    vals,
    att,
    done,
    send_sem,
    recv_sem,
):
    me = lax.axis_index("cells") if remote else 0
    if remote:
        enter(("cells",))
    spread_weights(w_ref, wide, proj_ref, proj_wide)
    lane = lax.broadcasted_iota(jnp.int32, (1, KEYS), 1)
    bias = jnp.where(lane < count_ref[0], 0.0, NEG).astype(F32)
    for h in range(HEADS):
        vals[KEYS * h : KEYS * h + KEYS, 128:256] = jnp.broadcast_to(ones_mask(h), (KEYS, 128))

    def column(f, _):
        x = x_ref[f]
        qkv[...] = mm(x, wide[...])
        for h in range(HEADS):
            at = 128 * (h // 4)
            rows = pl.ds(KEYS * h, KEYS)
            keys[rows, :] = qkv[0:KEYS, 256 + at : 384 + at].astype(BF16) * head_mask(h)
            vals[rows, 0:128] = qkv[0:KEYS, 512 + at : 640 + at].astype(BF16) * head_mask(h)
        for tile, pairs in ((0, (0, 2)), (1, (4,))):
            at = 128 * tile
            q = (qkv[:, at : at + 128] * QSCALE).astype(BF16)
            got = None
            for first in pairs:
                rows = pl.ds(KEYS * first, 2 * KEYS)
                score = mm(q, keys[rows, :], NT)
                probs = []
                for i in range(2):
                    s = score[:, KEYS * i : KEYS * i + KEYS] + bias
                    probs.append(jnp.exp2(s - jnp.max(s, axis=-1, keepdims=True)).astype(BF16))
                more = mm(jnp.concatenate(probs, axis=1), vals[rows, :])
                got = more if got is None else got + more
            att[:, at : at + 128] = (got[:, :128] / got[:, 128:]).astype(BF16)
        total = x.astype(F32) + mm(att[...], proj_wide[...])
        done[f] = layer_norm(total).astype(BF16)

        def to_peer(k, _):
            p = lax.rem(me + k, PEERS)
            source = done.at[f, pl.ds(pl.multiple_of(p * LOCAL, LOCAL), LOCAL), :]
            target = out_ref.at[me * OWN + f]
            if remote:

                @pl.when(k == 0)
                def _():
                    pltpu.make_async_copy(source, target, recv_sem).start()

                @pl.when(k != 0)
                def _():
                    pltpu.make_async_remote_copy(
                        src_ref=source,
                        dst_ref=target,
                        send_sem=send_sem,
                        recv_sem=recv_sem,
                        device_id={"cells": p},
                        device_id_type=MESH,
                    ).start()

            else:
                pltpu.make_async_copy(source, out_ref.at[p * OWN + f], recv_sem).start()
            return 0

        return lax.fori_loop(0, PEERS, to_peer, 0)

    lax.fori_loop(0, OWN, column, 0)
    pltpu.make_async_copy(out_ref, out_ref, recv_sem).wait()
    if remote:
        sent = out_ref.at[pl.ds(0, OWN * (PEERS - 1))]
        pltpu.make_async_copy(sent, sent, send_sem).wait()


def row_layer(columns, count, weight_qkv, weight_proj, remote=True):
    vmem = pl.BlockSpec(memory_space=pltpu.VMEM)
    return pl.pallas_call(
        functools.partial(row_kernel, remote),
        name="row_attention",
        out_shape=jax.ShapeDtypeStruct((FEATS, LOCAL, E), BF16),
        in_specs=[pl.BlockSpec(memory_space=pltpu.SMEM), vmem, vmem, vmem],
        out_specs=pl.BlockSpec(memory_space=pl.ANY),
        scratch_shapes=[
            pltpu.VMEM((E, 768), BF16),
            pltpu.VMEM((256, E), BF16),
            pltpu.VMEM((ROWS, 768), F32),
            pltpu.VMEM((HEADS * KEYS, 128), BF16),
            pltpu.VMEM((HEADS * KEYS, 256), BF16),
            pltpu.VMEM((ROWS, 256), BF16),
            pltpu.VMEM((OWN, ROWS, E), BF16),
            pltpu.SemaphoreType.DMA,
            pltpu.SemaphoreType.DMA,
        ],
        compiler_params=pltpu.CompilerParams(
            collective_id=1 if remote else None, has_side_effects=True, vmem_limit_bytes=VMEM_LIMIT
        ),
    )(count, columns, weight_qkv, weight_proj)


DROWS = 4
DTOK = DROWS * 128
HBLOCK = 256


def dense_kernel(
    x_ref, cot_ref, win_ref, wout_ref, out_ref, grad_ref, turn0, turn1, win_t, wout, wout_t, tok, cot, sums
):
    new = lax.broadcasted_iota(jnp.int32, (HID, HID), 0)
    old = lax.broadcasted_iota(jnp.int32, (HID, HID), 1)
    cell = new // 48
    table = (new - cell * 48) // 3
    place = table * 48 + cell * 3 + (new - cell * 48 - table * 3)
    perm = (old == place).astype(F32).astype(BF16)
    win_t[...] = mm(perm, win_ref[...], NT).astype(BF16)
    wout[...] = mm(perm, wout_ref[...], NT).astype(BF16)
    wout_t[...] = mm(wout_ref[...], perm, NT).astype(BF16)
    sums[...] = jnp.zeros(sums.shape, F32)
    tok[...] = jnp.zeros(tok.shape, BF16)
    cot[...] = jnp.zeros(cot.shape, BF16)
    ident = eye(E)

    def unpack(f, _):
        at = pl.multiple_of(f * STRIDE, 8)
        turn0[pl.ds(at, LOCAL), :] = x_ref[f, :, 0:128].astype(F32)
        turn1[pl.ds(at, LOCAL), 0:64] = x_ref[f, :, 128:192].astype(F32)
        return 0

    lax.fori_loop(0, FEATS, unpack, 0, unroll=4)

    def block(step, _):
        for j in range(DROWS):
            at = step * DROWS + j
            tok[128 * j : 128 * j + FEATS, 0:128] = turn0[pl.ds(at, FEATS, stride=STRIDE), :].astype(BF16)
            tok[128 * j : 128 * j + FEATS, 128:192] = turn1[pl.ds(at, FEATS, stride=STRIDE), 0:64].astype(BF16)
            cot[:, 128 * j : 128 * j + FEATS] = cot_ref[at]
        x = tok[...]
        c = cot[...]
        total = mm(ident, x, NT)
        for hb in range(HID // HBLOCK):
            rows = pl.ds(HBLOCK * hb, HBLOCK)
            pre = mm(win_t[rows, :], x, NT)
            cdf = 0.5 * lax.erf(pre * math.sqrt(0.5)) + 0.5
            act = (pre * cdf).astype(BF16)
            slope = cdf + pre * (jnp.exp2(pre * pre * (-0.5 * math.log2(math.e))) * (1.0 / math.sqrt(2 * math.pi)))
            dpre = (mm(wout[rows, :], c) * slope).astype(BF16)
            sums[0, rows, :] += mm(dpre, x)
            sums[1, rows, :] += mm(act, c, NT)
            total = total + mm(wout_t[:, HBLOCK * hb : HBLOCK * hb + HBLOCK], act)
        for j in range(DROWS):
            out_ref[step * DROWS + j] = total[:, 128 * j : 128 * j + FEATS].astype(BF16)
        return 0

    lax.fori_loop(0, LOCAL // DROWS, block, 0)
    factor = 1.0 / math.sqrt(16 * ROWS * FEATS)
    grad_ref[...] = (sums[...] * factor).astype(BF16)


def dense_layer(x, cot_t, w_in, w_out_t):
    vmem = pl.BlockSpec(memory_space=pltpu.VMEM)
    return pl.pallas_call(
        dense_kernel,
        name="feed_forward",
        out_shape=(
            jax.ShapeDtypeStruct((LOCAL, E, FEATS), BF16),
            jax.ShapeDtypeStruct((2, HID, E), BF16),
        ),
        in_specs=[vmem] * 4,
        out_specs=(vmem, vmem),
        scratch_shapes=[
            pltpu.VMEM((FEATS * STRIDE, 128), F32),
            pltpu.VMEM((FEATS * STRIDE, 128), F32),
            pltpu.VMEM((HID, E), BF16),
            pltpu.VMEM((HID, E), BF16),
            pltpu.VMEM((E, HID), BF16),
            pltpu.VMEM((DTOK, E), BF16),
            pltpu.VMEM((E, DTOK), BF16),
            pltpu.VMEM((2, HID, E), F32),
        ],
        compiler_params=pltpu.CompilerParams(vmem_limit_bytes=VMEM_LIMIT),
    )(x, cot_t, w_in, w_out_t)


def sums_kernel(part_ref, in_ref, out_ref, got, mid, got2, send_sem, recv_sem, send_sem2, recv_sem2):
    cell = lax.axis_index("cells")
    table = lax.axis_index("tables")
    enter(("cells", "tables"))

    def exchange(axis, me, source_of, landing, send_s, recv_s):
        @pl.loop(0, PEERS)
        def _(k):
            p = lax.rem(me + k, PEERS)

            @pl.when(k == 0)
            def _():
                pltpu.make_async_copy(source_of(p), landing.at[me], recv_s).start()

            @pl.when(k != 0)
            def _():
                pltpu.make_async_remote_copy(
                    src_ref=source_of(p),
                    dst_ref=landing.at[me],
                    send_sem=send_s,
                    recv_sem=recv_s,
                    device_id={axis: p},
                    device_id_type=MESH,
                ).start()

        pltpu.make_async_copy(landing, landing, recv_s).wait()
        sent = landing.at[pl.ds(0, PEERS - 1)]
        pltpu.make_async_copy(sent, sent, send_s).wait()

    exchange(
        "cells",
        cell,
        lambda p: part_ref.at[:, pl.ds(pl.multiple_of(48 * p, 16), 48), :],
        got,
        send_sem,
        recv_sem,
    )
    total = got[0].astype(F32)
    for p in range(1, PEERS):
        total = total + got[p].astype(F32)
    mid[...] = jnp.zeros(mid.shape, F32)
    for t in range(PEERS):
        mid[t, 0:3, :] = total[0, 3 * t : 3 * t + 3, :]
        mid[t, 4:7, :] = total[1, 3 * t : 3 * t + 3, :]
    exchange("tables", table, lambda p: mid.at[p], got2, send_sem2, recv_sem2)
    final = got2[0]
    for t in range(1, PEERS):
        final = final + got2[t]
    in_ref[...] = final[0:3, :]
    out_ref[...] = final[4:7, :]


def sum_grads(part):
    vmem = pl.BlockSpec(memory_space=pltpu.VMEM)
    return pl.pallas_call(
        sums_kernel,
        name="weight_gradient_sums",
        out_shape=(jax.ShapeDtypeStruct((3, E), F32), jax.ShapeDtypeStruct((3, E), F32)),
        in_specs=[vmem],
        out_specs=(vmem, vmem),
        scratch_shapes=[
            pltpu.VMEM((PEERS, 2, 48, E), BF16),
            pltpu.VMEM((PEERS, 8, E), F32),
            pltpu.VMEM((PEERS, 8, E), F32),
            pltpu.SemaphoreType.DMA,
            pltpu.SemaphoreType.DMA,
            pltpu.SemaphoreType.DMA,
            pltpu.SemaphoreType.DMA,
        ],
        compiler_params=pltpu.CompilerParams(
            collective_id=2, has_side_effects=True, vmem_limit_bytes=VMEM_LIMIT
        ),
    )(part)


def per_device(
    cells_in, train_count, feat_count, feat_qkv, feat_proj, row_qkv, row_proj, w_in, w_out, cotangent
):
    x_t = jnp.swapaxes(cells_in[0], 1, 2)
    cot_t = jnp.swapaxes(cotangent[0], 1, 2)
    columns = feature_layer(x_t, feat_count, feat_qkv, feat_proj)
    normed = row_layer(columns, train_count, row_qkv, row_proj)
    out_t, part = dense_layer(normed, cot_t, w_in, w_out.T)
    grad_in, grad_out = sum_grads(part)
    return (jnp.swapaxes(out_t, 1, 2)[None], grad_in.T, grad_out)


def solution(mesh):
    return jax.shard_map(
        per_device,
        mesh=mesh,
        in_specs=(
            P("tables", "cells", None, None),
            P("tables"),
            P("tables"),
            P(),
            P(),
            P(),
            P(),
            P(),
            P(),
            P("tables", "cells", None, None),
        ),
        out_specs=(
            P("tables", "cells", None, None),
            P(None, ("tables", "cells")),
            P(("tables", "cells"), None),
        ),
        check_vma=False,
    )
```

time: 413 us -> 122 us (0.30); the launches traced: 406 us -> 121 us
  matrix products: 135 us -> 0 us
  waiting for transfers between devices: 135 us -> 0 us
  Pallas kernels: 0 us -> 116 us
  local copies, waits for them, and re-layouts: 66.8 us -> 2.54 us
  other arithmetic: 27.8 us -> 0 us
  starting transfers between devices: 25.6 us -> 0 us
  between operations: 15.1 us -> 1.95 us
    pallas_call x0 -> x4, Pallas kernels: none -> 116 us  [the longest x1 38.2 us: feature_layer(): pl.pallas_call(functools.partial(feature_kernel, remote), name='feature_a...]
    dot_general x29 -> x0, matrix products: 98.8 us -> none  [the longest x1 27.8 us: dense_block(): pre = jnp.dot(normed, w_in, preferred_element_type=jnp.float32)]
    reduce_scatter x1 -> x0, waiting for transfers between devices: 86.2 us -> none  [sum_packed(): lax.psum_scatter(lines, axis, tiled=True).reshape(-1)]
    all_to_all x4 -> x0, waiting for transfers between devices: 49.2 us -> none  [the longest x1 24.5 us: per_device(): lax.all_to_all(grouped, 'cells', split_axis=1, concat_axis=0, tiled=True)]
    sub x7 -> x0, matrix products: 35.9 us -> none  [row_single(): probs = jax.nn.softmax(score, axis=-1).astype(jnp.bfloat16)]
    all_to_all x4 -> x0, starting transfers between devices: 25.6 us -> none  [the longest x2 12.9 us: sent_and_summed(): pieces = lax.all_to_all(split_up(x, dim, peers), axis, 0, 0, tiled=True)]
    reshape x8 -> x0, local copies, waits for them, and re-layouts: 22.7 us -> none  [the longest x1 9.68 us: feature_layer(): packed.astype(jnp.bfloat16).reshape(rows, feats, 3, HEADS, HEAD_DIM)]
    another operation x6 -> x0, local copies, waits for them, and re-layouts: 16.7 us -> none  [the longest x2 5.45 us: per_device(): grouped = mid.reshape(local_rows, groups, feats // groups, width)]
  transfers between devices with their start and end apart: 5 -> 0, of which waited for: 4 -> 0; matrix products, arithmetic and copies ran while one was open for 5% -> 0% of each run, Pallas kernels for 0% -> 0%
where the time goes in v1:
time: 122 us; the launch traced here: 121 us
  Pallas kernels  116 us (95%)
  local copies, waits for them, and re-layouts  2.54 us (2%)
  between operations  1.95 us (2%)
    pallas_call x1, Pallas kernels, feature_layer(): pl.pallas_call(functools.partial(feature_kernel, remote), name='feature_a...  38.2 us
    pallas_call x1, Pallas kernels, row_layer(): pl.pallas_call(functools.partial(row_kernel, remote), name='row_attention...  30.7 us
    pallas_call x1, Pallas kernels, sum_grads(): pl.pallas_call(sums_kernel, name='weight_gradient_sums', out_shape=(jax.S...  26.7 us
    pallas_call x1, Pallas kernels, dense_layer(): pl.pallas_call(dense_kernel, name='feed_forward', out_shape=(jax.ShapeDty...  20.5 us
    unnamed x2, local copies, waits for them, and re-layouts  2.54 us

profile of v1, /device:TPU:1, one launch (start us, length us, event | category | flops | bytes accessed | tf_op | source)
XLA Modules:
  0.0 120.6 jit_solution(16275960974753426073)
XLA Ops:
  1.9 38.2 %feature_attention.1.x_ref = bf16[7,512,192]{2,1,0:T(8,128)(2,1)} custom-call(s32[1]{0:T(128)S(6)} %copy.16.count_ref, bf16[32,192,112]{2,1,0:T(8,128)(2,1)} %bitcast.11, bf16[192,576]{1,0:T(8,128)(2,1)} %w_ref.2, bf16[192,192]{1,0:T(8,128)(2,1)} %proj_ref.2), custom_call_target="tpu_custom_call" | custom-call | tf_op jit(solution)/shard_map/feature_attention/pallas_call | solution.py:198
  40.1 30.7 %row_attention.1.x_ref = bf16[112,32,192]{2,1,0:T(8,128)(2,1)} custom-call(s32[1]{0:T(128)S(6)} %copy.15.count_ref, bf16[7,512,192]{2,1,0:T(8,128)(2,1)} %feature_attention.1.x_ref, bf16[192,576]{1,0:T(8,128)(2,1)} %w_ref.3, bf16[192,192]{1,0:T(8,128)(2,1)} %proj_ref.3), custom_call_target="tpu_custom_call" | custom-call | tf_op jit(solution)/shard_map/row_attention/pallas_call | solution.py:311
  70.8 20.5 %feed_forward.1 = (bf16[32,192,112]{2,1,0:T(8,128)(2,1)}, bf16[2,768,192]{2,1,0:T(8,128)(2,1)}) custom-call(bf16[112,32,192]{2,1,0:T(8,128)(2,1)} %row_attention.1.x_ref, bf16[32,192,112]{2,1,0:T(8,128)(2,1)} %bitcast.12, bf16[192,768]{1,0:T(8,128)(2,1)} %win_ref.1, bf16[192,768]{1,0:T(8,128)(2,1)} %bitcast.13), custom_call_target="tpu_custom_call" | custom-call | tf_op jit(solution)/shard_map/feed_forward/pallas_call | solution.py:394
  91.3 26.7 %weight_gradient_sums.1 = (f32[3,192]{1,0:T(4,128)}, f32[3,192]{1,0:T(4,128)}) custom-call(bf16[2,768,192]{2,1,0:T(8,128)(2,1)} %get-tuple-element.8.part_ref), custom_call_target="tpu_custom_call" | custom-call | tf_op jit(solution)/shard_map/weight_gradient_sums/pallas_call | solution.py:471
  118.1 1.3 %copy.17 = f32[192,3]{0,1:T(4,128)} copy(f32[192,3]{0,1:T(4,128)} %bitcast.14) | data formatting | bytes 4608
  119.4 1.3 %copy.18 = f32[3,192]{1,0:T(4,128)} copy(f32[3,192]{1,0:T(4,128)} %get-tuple-element.16) | data formatting | bytes 4608

commit v2 on v1

v2 whole, which is shorter than its diff:
```python
import functools
import math

import jax
import jax.numpy as jnp
from jax import lax
from jax.experimental import pallas as pl
from jax.experimental.pallas import tpu as pltpu
from jax.sharding import PartitionSpec as P

HEADS = 6
HEAD_DIM = 32
E = 192
HID = 768
FEATS = 112
ROWS = 512
LOCAL = 32
PEERS = 16
OWN = 7
KEYS = 384
STRIDE = 40
F32 = jnp.float32
BF16 = jnp.bfloat16
NEG = -1e30
QSCALE = math.log2(math.e) / math.sqrt(HEAD_DIM)
ATTENTION_VMEM = 60 * 1024 * 1024
DENSE_VMEM = 60 * 1024 * 1024
SUMS_VMEM = 8 * 1024 * 1024
MESH = pl.DeviceIdType.MESH

NN = (((1,), (0,)), ((), ()))
NT = (((1,), (1,)), ((), ()))


def mm(a, b, dims=NN):
    return lax.dot_general(a, b, dims, preferred_element_type=F32)


def eye(n):
    r = lax.broadcasted_iota(jnp.int32, (n, n), 0)
    c = lax.broadcasted_iota(jnp.int32, (n, n), 1)
    return (r == c).astype(F32).astype(BF16)


def head_mask(head):
    lane = lax.broadcasted_iota(jnp.int32, (1, 128), 1)
    low = 32 * (head % 4)
    return ((lane >= low) & (lane < low + 32)).astype(F32).astype(BF16)


def ones_mask(head):
    lane = lax.broadcasted_iota(jnp.int32, (1, 128), 1)
    low = 32 * (head % 4)
    high = 128 if head == 5 else low + 32
    return ((lane >= low) & (lane < high)).astype(F32).astype(BF16)


def spread_weights(w_ref, wide_ref, proj_ref, proj_wide):
    wide_ref[...] = jnp.zeros(wide_ref.shape, BF16)
    for part in range(3):
        wide_ref[0:192, 256 * part : 256 * part + 192] = w_ref[:, 192 * part : 192 * part + 192]
    proj_wide[...] = jnp.zeros(proj_wide.shape, BF16)
    proj_wide[0:192, 0:192] = proj_ref[...]


def layer_norm(low, high):
    mean = (jnp.sum(low, axis=-1, keepdims=True) + jnp.sum(high, axis=-1, keepdims=True)) * (1.0 / E)
    low = low - mean
    half = lax.broadcasted_iota(jnp.int32, (1, 128), 1) < 64
    high = jnp.where(half, high - mean, 0.0)
    var = jnp.sum(low * low + high * high, axis=-1, keepdims=True) * (1.0 / E)
    scale = lax.rsqrt(var + 1e-05)
    return low * scale, high * scale


def greet(axes):
    barrier = pltpu.get_barrier_semaphore()
    for axis in axes:
        me = lax.axis_index(axis)

        @pl.loop(1, PEERS)
        def _(k):
            pl.semaphore_signal(
                barrier, inc=1, device_id={axis: lax.rem(me + k, PEERS)}, device_id_type=MESH
            )


def await_peers(axes):
    pl.semaphore_wait(pltpu.get_barrier_semaphore(), (PEERS - 1) * len(axes))


FBLOCK = 4
TILES = 11


def attention_kernel(
    remote,
    feat_count,
    train_count,
    x_ref,
    fw_ref,
    fproj_ref,
    rw_ref,
    rproj_ref,
    out_ref,
    fwide,
    fproj,
    rwide,
    rproj,
    tok,
    qkv,
    vals0,
    vals1,
    att,
    turn0,
    turn1,
    send,
    cols,
    rq,
    rkv,
    keys,
    vals,
    ratt,
    done,
    send_sem,
    cols_sem,
    send2_sem,
    recv2_sem,
):
    me = lax.axis_index("cells") if remote else 0
    if remote:
        greet(("cells",))
    spread_weights(fw_ref, fwide, fproj_ref, fproj)
    ident = eye(FEATS)
    tok[:, 192:256] = jnp.zeros((FBLOCK * FEATS, 64), F32)
    lane = lax.broadcasted_iota(jnp.int32, (1, 128), 1)
    bias = jnp.where(lane < feat_count[0], 0.0, NEG).astype(F32)
    for ref, heads in ((vals0, range(4)), (vals1, range(4, 6))):
        ref[...] = jnp.zeros(ref.shape, BF16)
        for j in range(FBLOCK):
            for i, h in enumerate(heads):
                ref[j, 128 * i : 128 * i + FEATS, 128:256] = jnp.broadcast_to(ones_mask(h), (FEATS, 128))
    zero_pad = jnp.zeros((128 - FEATS, 128), BF16)

    def block(step, _):
        for j in range(FBLOCK):
            tok[pl.ds(FEATS * j, FEATS), 0:192] = mm(ident, x_ref[step * FBLOCK + j], NT)
        qkv[...] = mm(tok[...].astype(BF16), fwide[...])
        for j in range(FBLOCK):
            rows = pl.ds(FEATS * j, FEATS)
            for tile, heads, ref in ((0, range(4), vals0), (1, range(4, 6), vals1)):
                at = 128 * tile
                q = (qkv[rows, at : at + 128] * QSCALE).astype(BF16)
                k = qkv[rows, 256 + at : 384 + at].astype(BF16)
                v = qkv[rows, 512 + at : 640 + at].astype(BF16)
                pieces = []
                for i, h in enumerate(heads):
                    pieces += [k * head_mask(h), zero_pad]
                    ref[j, 128 * i : 128 * i + FEATS, 0:128] = v * head_mask(h)
                score = mm(q, jnp.concatenate(pieces, axis=0), NT)
                probs = []
                for i, h in enumerate(heads):
                    s = score[:, 128 * i : 128 * i + 128] + bias
                    probs.append(jnp.exp2(s - jnp.max(s, axis=-1, keepdims=True)).astype(BF16))
                got = mm(jnp.concatenate(probs, axis=1), ref[j])
                att[rows, at : at + 128] = (got[:, :128] / got[:, 128:]).astype(BF16)
        mixed = mm(att[...], fproj[...])
        low, high = layer_norm(tok[:, 0:128] + mixed[:, 0:128], tok[:, 128:256] + mixed[:, 128:256])
        for j in range(FBLOCK):
            at = step * FBLOCK + j
            turn0[pl.ds(at, FEATS, stride=STRIDE), :] = low[FEATS * j : FEATS * j + FEATS]
            turn1[pl.ds(at, FEATS, stride=STRIDE), :] = high[FEATS * j : FEATS * j + FEATS]
        return 0

    def pack(p, group, base):
        def rows_of(ref, f):
            return ref[pl.ds(pl.multiple_of((p * OWN + f) * STRIDE + base, 8), 16), :]

        f = 2 * group
        at = 3 * group
        send[p, at, pl.ds(base, 16), :] = rows_of(turn0, f).astype(BF16)
        high = rows_of(turn1, f)
        if f + 1 < OWN:
            at += 1
            send[p, at, pl.ds(base, 16), :] = rows_of(turn0, f + 1).astype(BF16)
            high = high + pltpu.roll(rows_of(turn1, f + 1), 64, 1)
        send[p, at + 1, pl.ds(base, 16), :] = high.astype(BF16)

    def pass_on(source, target, k, axis, p, send_s, recv_s):
        if not remote:
            pltpu.make_async_copy(source, target, recv_s).start()
            return

        @pl.when(k == 0)
        def _():
            pltpu.make_async_copy(source, target, recv_s).start()

        @pl.when(k != 0)
        def _():
            pltpu.make_async_remote_copy(
                src_ref=source,
                dst_ref=target,
                send_sem=send_s,
                recv_sem=recv_s,
                device_id={axis: p},
                device_id_type=MESH,
            ).start()

    def place(p):
        return pl.multiple_of((me if remote else p) * LOCAL, LOCAL)

    lax.fori_loop(0, 16 // FBLOCK, block, 0)
    if remote:
        await_peers(("cells",))

    def first_half(k, _):
        p = lax.rem(me + k, PEERS)
        for group in range(4):
            pack(p, group, 0)
        pass_on(
            send.at[p, :, pl.ds(0, 16), :],
            cols.at[:, pl.ds(place(p), 16), :],
            k,
            "cells",
            p,
            send_sem,
            cols_sem.at[4],
        )
        return 0

    lax.fori_loop(0, PEERS, first_half, 0)
    lax.fori_loop(16 // FBLOCK, 32 // FBLOCK, block, 0)
    for group in range(4):
        tiles = pl.ds(3 * group, min(3, TILES - 3 * group))

        def second_half(k, _):
            p = lax.rem(me + k, PEERS)
            pack(p, group, 16)
            pass_on(
                send.at[p, tiles, pl.ds(16, 16), :],
                cols.at[tiles, pl.ds(place(p) + 16, 16), :],
                k,
                "cells",
                p,
                send_sem,
                cols_sem.at[group],
            )
            return 0

        lax.fori_loop(0, PEERS, second_half, 0)

    spread_weights(rw_ref, rwide, rproj_ref, rproj)
    lane = lax.broadcasted_iota(jnp.int32, (1, KEYS), 1)
    rbias = jnp.where(lane < train_count[0], 0.0, NEG).astype(F32)
    for h in range(HEADS):
        vals[KEYS * h : KEYS * h + KEYS, 128:256] = jnp.broadcast_to(ones_mask(h), (KEYS, 128))
    half_lane = lax.broadcasted_iota(jnp.int32, (1, 128), 1) < 64

    def column(f, _):
        @pl.when(f == 0)
        def _():
            ref = cols.at[:, pl.ds(0, ROWS // 2), :]
            pltpu.make_async_copy(ref, ref, cols_sem.at[4]).wait()

        for group in range(4):

            @pl.when(f == 2 * group)
            def _():
                ref = cols.at[pl.ds(3 * group, min(3, TILES - 3 * group)), pl.ds(0, ROWS // 2), :]
                pltpu.make_async_copy(ref, ref, cols_sem.at[group]).wait()

        odd = lax.rem(f, 2)
        at = 3 * (f // 2)
        low = cols[at + odd]
        high = cols[jnp.minimum(at + 2, TILES - 1)].astype(F32)
        high = jnp.where(half_lane, pltpu.roll(high, 64 * odd, 1), 0.0)
        x = jnp.concatenate([low, high.astype(BF16)], axis=1)
        rq[...] = (mm(x, rwide[:, 0:256]) * QSCALE).astype(BF16)
        rkv[...] = mm(x[0:KEYS], rwide[:, 256:768]).astype(BF16)
        for h in range(HEADS):
            at = 128 * (h // 4)
            rows = pl.ds(KEYS * h, KEYS)
            keys[rows, :] = rkv[:, at : at + 128] * head_mask(h)
            vals[rows, 0:128] = rkv[:, 256 + at : 384 + at] * head_mask(h)
        for tile, pairs in ((0, (0, 2)), (1, (4,))):
            at = 128 * tile
            got = None
            for first in pairs:
                rows = pl.ds(KEYS * first, 2 * KEYS)
                score = mm(rq[:, at : at + 128], keys[rows, :], NT)
                probs = []
                for i in range(2):
                    s = score[:, KEYS * i : KEYS * i + KEYS] + rbias
                    probs.append(jnp.exp2(s - jnp.max(s, axis=-1, keepdims=True)).astype(BF16))
                more = mm(jnp.concatenate(probs, axis=1), vals[rows, :])
                got = more if got is None else got + more
            ratt[:, at : at + 128] = (got[:, :128] / got[:, 128:]).astype(BF16)
        mixed = mm(ratt[...], rproj[...])
        low, high = layer_norm(low.astype(F32) + mixed[:, 0:128], high + mixed[:, 128:256])
        done[f, :, 0:32, :] = low.astype(BF16).reshape(PEERS, 32, 128)
        high = high.reshape(PEERS, 2, 16, 128)
        high = high[:, 0] + pltpu.roll(high[:, 1].reshape(PEERS * 16, 128), 64, 1).reshape(PEERS, 16, 128)
        done[f, :, 32:48, :] = high.astype(BF16)

        def to_peer(k, _):
            p = lax.rem(me + k, PEERS)
            pass_on(
                done.at[f, p],
                out_ref.at[(me if remote else p) * OWN + f],
                k,
                "cells",
                p,
                send2_sem,
                recv2_sem,
            )
            return 0

        return lax.fori_loop(0, PEERS, to_peer, 0)

    lax.fori_loop(0, OWN, column, 0)
    if remote:
        sent = send.at[pl.ds(0, PEERS - 1)]
        pltpu.make_async_copy(sent, sent, send_sem).wait()
        sent = out_ref.at[pl.ds(0, OWN * (PEERS - 1))]
        pltpu.make_async_copy(sent, sent, send2_sem).wait()
    pltpu.make_async_copy(out_ref, out_ref, recv2_sem).wait()


def attention_layers(x_t, feat_count, train_count, feat_qkv, feat_proj, row_qkv, row_proj, remote=True):
    vmem = pl.BlockSpec(memory_space=pltpu.VMEM)
    smem = pl.BlockSpec(memory_space=pltpu.SMEM)
    return pl.pallas_call(
        functools.partial(attention_kernel, remote),
        name="attention",
        out_shape=jax.ShapeDtypeStruct((FEATS, 48, 128), BF16),
        in_specs=[smem, smem] + [vmem] * 5,
        out_specs=pl.BlockSpec(memory_space=pl.ANY),
        scratch_shapes=[
            pltpu.VMEM((256, 768), BF16),
            pltpu.VMEM((256, 256), BF16),
            pltpu.VMEM((256, 768), BF16),
            pltpu.VMEM((256, 256), BF16),
            pltpu.VMEM((FBLOCK * FEATS, 256), F32),
            pltpu.VMEM((FBLOCK * FEATS, 768), F32),
            pltpu.VMEM((FBLOCK, 512, 256), BF16),
            pltpu.VMEM((FBLOCK, 256, 256), BF16),
            pltpu.VMEM((FBLOCK * FEATS, 256), BF16),
            pltpu.VMEM((FEATS * STRIDE, 128), F32),
            pltpu.VMEM((FEATS * STRIDE, 128), F32),
            pltpu.VMEM((PEERS, TILES, LOCAL, 128), BF16),
            pltpu.VMEM((TILES, ROWS, 128), BF16),
            pltpu.VMEM((ROWS, 256), BF16),
            pltpu.VMEM((KEYS, 512), BF16),
            pltpu.VMEM((HEADS * KEYS, 128), BF16),
            pltpu.VMEM((HEADS * KEYS, 256), BF16),
            pltpu.VMEM((ROWS, 256), BF16),
            pltpu.VMEM((OWN, PEERS, 48, 128), BF16),
            pltpu.SemaphoreType.DMA,
            pltpu.SemaphoreType.DMA((5,)),
            pltpu.SemaphoreType.DMA,
            pltpu.SemaphoreType.DMA,
        ],
        compiler_params=pltpu.CompilerParams(
            collective_id=0 if remote else None, has_side_effects=True, vmem_limit_bytes=ATTENTION_VMEM
        ),
    )(feat_count, train_count, x_t, feat_qkv, feat_proj, row_qkv, row_proj)


DROWS = 4
DTOK = DROWS * 128
HBLOCK = 256


def dense_kernel(
    x_ref, cot_ref, win_ref, wout_ref, out_ref, grad_ref, turn0, turn1, win_t, wout, wout_t, tok, cot, sums
):
    new = lax.broadcasted_iota(jnp.int32, (HID, 1), 0)
    old = lax.broadcasted_iota(jnp.int32, (HID, HID), 1)
    core = new // 384
    chip = (new - core * 384) // 48
    within = new - core * 384 - chip * 48
    table = within // 3
    place = table * 48 + (2 * chip + core) * 3 + (within - table * 3)
    perm = (old == place).astype(F32).astype(BF16)
    win_t[...] = mm(perm, win_ref[...], NT).astype(BF16)
    wout[...] = (0.5 * mm(perm, wout_ref[...], NT)).astype(BF16)
    wout_t[...] = (0.5 * mm(wout_ref[...], perm, NT)).astype(BF16)
    sums[...] = jnp.zeros(sums.shape, F32)
    tok[...] = jnp.zeros(tok.shape, BF16)
    cot[...] = jnp.zeros(cot.shape, BF16)
    ident = eye(E)

    def unpack(f, _):
        at = pl.multiple_of(f * STRIDE, 8)
        turn0[pl.ds(at, LOCAL), :] = x_ref[f, 0:32, :].astype(F32)
        high = x_ref[f, 32:48, :].astype(F32)
        turn1[pl.ds(at, 16), :] = high
        turn1[pl.ds(at + 16, 16), :] = pltpu.roll(high, 64, 1)
        return 0

    lax.fori_loop(0, FEATS, unpack, 0, unroll=4)

    def block(step, _):
        for j in range(DROWS):
            at = step * DROWS + j
            tok[128 * j : 128 * j + FEATS, 0:128] = turn0[pl.ds(at, FEATS, stride=STRIDE), :].astype(BF16)
            tok[128 * j : 128 * j + FEATS, 128:192] = turn1[pl.ds(at, FEATS, stride=STRIDE), 0:64].astype(BF16)
            cot[:, 128 * j : 128 * j + FEATS] = cot_ref[at]
        x = tok[...]
        c = cot[...]
        total = mm(ident, x, NT)
        for hb in range(HID // HBLOCK):
            rows = pl.ds(HBLOCK * hb, HBLOCK)
            pre = mm(win_t[rows, :], x, NT)
            u = pre * math.sqrt(0.5)
            twice = lax.erf(u) + 1.0
            act = (pre * twice).astype(BF16)
            slope = twice + u * jnp.exp2(math.log2(2.0 / math.sqrt(math.pi)) - (u * u) * math.log2(math.e))
            dpre = (mm(wout[rows, :], c) * slope).astype(BF16)
            sums[0, rows, :] += mm(dpre, x)
            sums[1, rows, :] += mm(act, c, NT)
            total = total + mm(wout_t[:, HBLOCK * hb : HBLOCK * hb + HBLOCK], act)
        for j in range(DROWS):
            out_ref[step * DROWS + j] = total[:, 128 * j : 128 * j + FEATS].astype(BF16)
        return 0

    lax.fori_loop(0, LOCAL // DROWS, block, 0)
    factor = 1.0 / math.sqrt(16 * ROWS * FEATS)
    grad_ref[0] = (sums[0, :, 0:128] * factor).astype(BF16)
    grad_ref[1] = (sums[1, :, 0:128] * (0.5 * factor)).astype(BF16)
    grad_ref[2, :, 0:64] = (sums[0, :, 128:192] * factor).astype(BF16)
    grad_ref[2, :, 64:128] = (sums[1, :, 128:192] * (0.5 * factor)).astype(BF16)


def dense_layer(x, cot_t, w_in, w_out_t):
    vmem = pl.BlockSpec(memory_space=pltpu.VMEM)
    return pl.pallas_call(
        dense_kernel,
        name="feed_forward",
        out_shape=(
            jax.ShapeDtypeStruct((LOCAL, E, FEATS), BF16),
            jax.ShapeDtypeStruct((3, HID, 128), BF16),
        ),
        in_specs=[vmem] * 4,
        out_specs=(vmem, vmem),
        scratch_shapes=[
            pltpu.VMEM((FEATS * STRIDE, 128), F32),
            pltpu.VMEM((FEATS * STRIDE, 128), F32),
            pltpu.VMEM((HID, E), BF16),
            pltpu.VMEM((HID, E), BF16),
            pltpu.VMEM((E, HID), BF16),
            pltpu.VMEM((DTOK, E), BF16),
            pltpu.VMEM((E, DTOK), BF16),
            pltpu.VMEM((2, HID, E), F32),
        ],
        compiler_params=pltpu.CompilerParams(vmem_limit_bytes=DENSE_VMEM),
    )(x, cot_t, w_in, w_out_t)


CHIPS = PEERS // 2


def sums_kernel(part_ref, in_ref, out_ref, pair, half, got, mid, row, got2, sems):
    cell = lax.axis_index("cells")
    table = lax.axis_index("tables")
    chip = cell // 2
    core = cell - 2 * chip
    greet(("cells", "tables"))
    await_peers(("cells", "tables"))

    theirs = pl.ds(pl.multiple_of((1 - core) * 384, 384), 384)
    mine = pl.ds(pl.multiple_of(core * 384, 384), 384)
    swap = pltpu.make_async_remote_copy(
        src_ref=part_ref.at[:, theirs, :],
        dst_ref=pair,
        send_sem=sems.at[0],
        recv_sem=sems.at[1],
        device_id={"cells": 2 * chip + 1 - core},
        device_id_type=MESH,
    )
    swap.start()
    swap.wait()
    for t in range(3):
        half[t] = (part_ref[t, mine, :].astype(F32) + pair[t].astype(F32)).astype(BF16)

    def exchange(count, me, axis, place_of, source_of, landing, send_s, recv_s):
        @pl.loop(0, count)
        def _(k):
            p = lax.rem(me + k, count)

            @pl.when(k == 0)
            def _():
                pltpu.make_async_copy(source_of(p), landing.at[me], recv_s).start()

            @pl.when(k != 0)
            def _():
                pltpu.make_async_remote_copy(
                    src_ref=source_of(p),
                    dst_ref=landing.at[me],
                    send_sem=send_s,
                    recv_sem=recv_s,
                    device_id={axis: place_of(p)},
                    device_id_type=MESH,
                ).start()

        pltpu.make_async_copy(landing, landing, recv_s).wait()

    exchange(
        CHIPS,
        chip,
        "cells",
        lambda p: 2 * p + core,
        lambda p: half.at[:, pl.ds(pl.multiple_of(48 * p, 16), 48), :],
        got,
        sems.at[2],
        sems.at[3],
    )
    total = got[0].astype(F32)
    for p in range(1, CHIPS):
        total = total + got[p].astype(F32)
    mid[...] = jnp.zeros(mid.shape, F32)
    for t in range(PEERS):
        for i in range(3):
            mid[t, 4 * i : 4 * i + 3, :] = total[i, 3 * t : 3 * t + 3, :]
    row[...] = mid[...].astype(BF16)
    exchange(PEERS, table, "tables", lambda p: p, lambda p: row.at[p], got2, sems.at[4], sems.at[5])
    final = got2[0].astype(F32)
    for t in range(1, PEERS):
        final = final + got2[t].astype(F32)
    in_ref[:, 0:128] = final[0:3, :]
    in_ref[:, 128:192] = final[8:11, 0:64]
    out_ref[:, 0:128] = final[4:7, :]
    out_ref[:, 128:192] = final[8:11, 64:128]
    sent = got.at[pl.ds(0, CHIPS - 1)]
    pltpu.make_async_copy(sent, sent, sems.at[2]).wait()
    sent = got2.at[pl.ds(0, PEERS - 1)]
    pltpu.make_async_copy(sent, sent, sems.at[4]).wait()


def sum_grads(part):
    vmem = pl.BlockSpec(memory_space=pltpu.VMEM)
    return pl.pallas_call(
        sums_kernel,
        name="weight_gradient_sums",
        out_shape=(jax.ShapeDtypeStruct((3, E), F32), jax.ShapeDtypeStruct((3, E), F32)),
        in_specs=[vmem],
        out_specs=(vmem, vmem),
        scratch_shapes=[
            pltpu.VMEM((3, 384, 128), BF16),
            pltpu.VMEM((3, 384, 128), BF16),
            pltpu.VMEM((CHIPS, 3, 48, 128), BF16),
            pltpu.VMEM((PEERS, 16, 128), F32),
            pltpu.VMEM((PEERS, 16, 128), BF16),
            pltpu.VMEM((PEERS, 16, 128), BF16),
            pltpu.SemaphoreType.DMA((6,)),
        ],
        compiler_params=pltpu.CompilerParams(
            collective_id=2, has_side_effects=True, vmem_limit_bytes=SUMS_VMEM
        ),
    )(part)


def per_device(
    cells_in, train_count, feat_count, feat_qkv, feat_proj, row_qkv, row_proj, w_in, w_out, cotangent
):
    x_t = jnp.swapaxes(cells_in[0], 1, 2)
    cot_t = jnp.swapaxes(cotangent[0], 1, 2)
    normed = attention_layers(x_t, feat_count, train_count, feat_qkv, feat_proj, row_qkv, row_proj)
    out_t, part = dense_layer(normed, cot_t, w_in, w_out.T)
    grad_in, grad_out = sum_grads(part)
    return (jnp.swapaxes(out_t, 1, 2)[None], grad_in.T, grad_out)


def solution(mesh):
    return jax.shard_map(
        per_device,
        mesh=mesh,
        in_specs=(
            P("tables", "cells", None, None),
            P("tables"),
            P("tables"),
            P(),
            P(),
            P(),
            P(),
            P(),
            P(),
            P("tables", "cells", None, None),
        ),
        out_specs=(
            P("tables", "cells", None, None),
            P(None, ("tables", "cells")),
            P(("tables", "cells"), None),
        ),
        check_vma=False,
    )
```

time: 122 us -> 102 us (0.84)
  Pallas kernels: 116 us -> 97.3 us
    pallas_call x2 -> x1, Pallas kernels: 68.9 us -> 53.3 us  [attention_layers(): pl.pallas_call(functools.partial(attention_kernel, remote), name='attenti...]
    pallas_call x1, Pallas kernels: 26.7 us -> 20.7 us  [sum_grads(): pl.pallas_call(sums_kernel, name='weight_gradient_sums', out_shape=(jax.S...]
    pallas_call x1, Pallas kernels: 20.5 us -> 23.3 us  [dense_layer(): pl.pallas_call(dense_kernel, name='feed_forward', out_shape=(jax.ShapeDty...]
    unnamed x2 -> x4, local copies, waits for them, and re-layouts: 2.54 us -> 2.25 us
where the time goes in v2:
time: 102 us
  Pallas kernels  97.3 us (95%)
  local copies, waits for them, and re-layouts  2.25 us (2%)
  between operations  1.94 us (2%)
    pallas_call x1, Pallas kernels, attention_layers(): pl.pallas_call(functools.partial(attention_kernel, remote), name='attenti...  53.3 us
    pallas_call x1, Pallas kernels, dense_layer(): pl.pallas_call(dense_kernel, name='feed_forward', out_shape=(jax.ShapeDty...  23.3 us
    pallas_call x1, Pallas kernels, sum_grads(): pl.pallas_call(sums_kernel, name='weight_gradient_sums', out_shape=(jax.S...  20.7 us
    unnamed x4, local copies, waits for them, and re-layouts  2.25 us

profile of v2, /device:TPU:1, one launch (start us, length us, event | category | flops | bytes accessed | tf_op | source)
XLA Modules:
  0.0 101.5 jit_solution(11153222542308981888)
XLA Ops:
  1.9 53.3 %attention.1.x_ref = bf16[112,48,128]{2,1,0:T(8,128)(2,1)} custom-call(s32[1]{0:T(128)S(6)} %copy.16.feat_count, s32[1]{0:T(128)S(6)} %copy.15.train_count, bf16[32,192,112]{2,1,0:T(8,128)(2,1)} %bitcast.13, bf16[192,576]{1,0:T(8,128)(2,1)} %fw_ref.1, bf16[192,192]{1,0:T(8,128)(2,1)} %fproj_ref.1, bf16[192,576]{1,0:T(8,128)(2,1)} %rw_ref.1, ...), custom_call_target="tpu_custom_call" | custom-call | tf_op jit(solution)/shard_map/attention/pallas_call | solution.py:332
  55.3 23.3 %feed_forward.1 = (bf16[32,192,112]{2,1,0:T(8,128)(2,1)}, bf16[3,768,128]{2,1,0:T(8,128)(2,1)}) custom-call(bf16[112,48,128]{2,1,0:T(8,128)(2,1)} %attention.1.x_ref, bf16[32,192,112]{2,1,0:T(8,128)(2,1)} %bitcast.12, bf16[192,768]{1,0:T(8,128)(2,1)} %win_ref.1, bf16[192,768]{1,0:T(8,128)(2,1)} %bitcast.14), custom_call_target="tpu_custom_call" | custom-call | tf_op jit(solution)/shard_map/feed_forward/pallas_call | solution.py:437
  78.5 0.0 copy-start
  78.5 1.1 %copy-done = bf16[3,768,128]{2,1,0:T(8,128)(2,1)S(1)} copy-done((bf16[3,768,128]{2,1,0:T(8,128)(2,1)S(1)}, bf16[3,768,128]{2,1,0:T(8,128)(2,1)}, u32[]{:S(2)}) %copy-start) | copy-done | bytes 589848
  79.6 20.7 %weight_gradient_sums.1 = (f32[3,192]{1,0:T(4,128)S(1)}, f32[3,192]{1,0:T(4,128)S(1)}) custom-call(bf16[3,768,128]{2,1,0:T(8,128)(2,1)S(1)} %copy-done), custom_call_target="tpu_custom_call" | custom-call | tf_op jit(solution)/shard_map/weight_gradient_sums/pallas_call | solution.py:542
  100.3 0.6 copy.17
  100.9 0.6 copy.18
Async XLA Ops:
  78.5 1.1 %copy-start = (bf16[3,768,128]{2,1,0:T(8,128)(2,1)S(1)}, bf16[3,768,128]{2,1,0:T(8,128)(2,1)}, u32[]{:S(2)}) copy-start(bf16[3,768,128]{2,1,0:T(8,128)(2,1)} %get-tuple-element.8.part_ref) | copy-start | bytes 1769476

commit v3 on v2

v3 whole, which is shorter than its diff:
```python
import functools
import math

import jax
import jax.numpy as jnp
from jax import lax
from jax.experimental import pallas as pl
from jax.experimental.pallas import tpu as pltpu
from jax.sharding import PartitionSpec as P

HEADS = 6
HEAD_DIM = 32
E = 192
HID = 768
FEATS = 112
ROWS = 512
LOCAL = 32
PEERS = 16
OWN = 7
KEYS = 384
STRIDE = 40
F32 = jnp.float32
BF16 = jnp.bfloat16
NEG = -1e30
QSCALE = math.log2(math.e) / math.sqrt(HEAD_DIM)
VMEM_LIMIT = 60 * 1024 * 1024
MESH = pl.DeviceIdType.MESH

NN = (((1,), (0,)), ((), ()))
NT = (((1,), (1,)), ((), ()))


def mm(a, b, dims=NN):
    return lax.dot_general(a, b, dims, preferred_element_type=F32)


def eye(n):
    r = lax.broadcasted_iota(jnp.int32, (n, n), 0)
    c = lax.broadcasted_iota(jnp.int32, (n, n), 1)
    return (r == c).astype(F32).astype(BF16)


def head_mask(head):
    lane = lax.broadcasted_iota(jnp.int32, (1, 128), 1)
    low = 32 * (head % 4)
    return ((lane >= low) & (lane < low + 32)).astype(F32).astype(BF16)


def ones_mask(head):
    lane = lax.broadcasted_iota(jnp.int32, (1, 128), 1)
    low = 32 * (head % 4)
    high = 128 if head == 5 else low + 32
    return ((lane >= low) & (lane < high)).astype(F32).astype(BF16)


def spread_weights(w_ref, wide_ref, proj_ref, proj_wide):
    wide_ref[...] = jnp.zeros(wide_ref.shape, BF16)
    for part in range(3):
        wide_ref[0:192, 256 * part : 256 * part + 192] = w_ref[:, 192 * part : 192 * part + 192]
    proj_wide[...] = jnp.zeros(proj_wide.shape, BF16)
    proj_wide[0:192, 0:192] = proj_ref[...]


def layer_norm(low, high):
    mean = (jnp.sum(low, axis=-1, keepdims=True) + jnp.sum(high, axis=-1, keepdims=True)) * (1.0 / E)
    low = low - mean
    half = lax.broadcasted_iota(jnp.int32, (1, 128), 1) < 64
    high = jnp.where(half, high - mean, 0.0)
    var = jnp.sum(low * low + high * high, axis=-1, keepdims=True) * (1.0 / E)
    scale = lax.rsqrt(var + 1e-05)
    return low * scale, high * scale


def greet(axes):
    barrier = pltpu.get_barrier_semaphore()
    for axis in axes:
        me = lax.axis_index(axis)

        @pl.loop(1, PEERS)
        def _(k):
            pl.semaphore_signal(
                barrier, inc=1, device_id={axis: lax.rem(me + k, PEERS)}, device_id_type=MESH
            )


def await_peers(axes):
    pl.semaphore_wait(pltpu.get_barrier_semaphore(), (PEERS - 1) * len(axes))


DROWS = 4
DTOK = DROWS * 128
HBLOCK = 256
CHIPS = PEERS // 2


def order_hidden(win_ref, wout_ref, win_t, wout, wout_t):
    new = lax.broadcasted_iota(jnp.int32, (HID, 1), 0)
    old = lax.broadcasted_iota(jnp.int32, (HID, HID), 1)
    core = new // 384
    chip = (new - core * 384) // 48
    within = new - core * 384 - chip * 48
    table = within // 3
    place = table * 48 + (2 * chip + core) * 3 + (within - table * 3)
    perm = (old == place).astype(F32).astype(BF16)
    win_t[...] = mm(perm, win_ref[...], NT).astype(BF16)
    wout[...] = (0.5 * mm(perm, wout_ref[...], NT)).astype(BF16)
    wout_t[...] = (0.5 * mm(wout_ref[...], perm, NT)).astype(BF16)


def feed_forward(step, cot_ref, turn0, turn1, win_t, wout, wout_t, tok, cot, sums, out_buf):
    for j in range(DROWS):
        at = step * DROWS + j
        tok[128 * j : 128 * j + FEATS, 0:128] = turn0[pl.ds(at, FEATS, stride=STRIDE), :].astype(BF16)
        tok[128 * j : 128 * j + FEATS, 128:192] = turn1[pl.ds(at, FEATS, stride=STRIDE), 0:64].astype(BF16)
        cot[:, 128 * j : 128 * j + FEATS] = cot_ref[at]
    x = tok[...]
    c = cot[...]
    total = mm(eye(E), x, NT)
    waiting = []
    for n in range(HID // HBLOCK + 1):
        if n < HID // HBLOCK:
            rows = pl.ds(HBLOCK * n, HBLOCK)
            waiting.append((mm(win_t[rows, :], x, NT), mm(wout[rows, :], c)))
        if n:
            pre, dact = waiting.pop(0)
            begin = HBLOCK * (n - 1)
            rows = pl.ds(begin, HBLOCK)
            u = pre * math.sqrt(0.5)
            twice = lax.erf(u) + 1.0
            act = (pre * twice).astype(BF16)
            slope = twice + u * jnp.exp2(math.log2(2.0 / math.sqrt(math.pi)) - (u * u) * math.log2(math.e))
            dpre = (dact * slope).astype(BF16)
            sums[0, rows, :] += mm(dpre, x)
            sums[1, rows, :] += mm(act, c, NT)
            total = total + mm(wout_t[:, begin : begin + HBLOCK], act)
    for j in range(DROWS):
        out_buf[step * DROWS + j] = total[:, 128 * j : 128 * j + FEATS].astype(BF16)


FBLOCK = 4
TILES = 11
CHUNK = 256
LAG = 2


def layer_kernel(
    remote,
    feat_count,
    train_count,
    x_hbm,
    fw_ref,
    fproj_ref,
    rw_ref,
    rproj_ref,
    win_ref,
    wout_ref,
    cot_hbm,
    out_hbm,
    grad_in_ref,
    grad_out_ref,
    fwide,
    fproj,
    rwide,
    rproj,
    tok,
    kept,
    qkv,
    vals0,
    vals1,
    att,
    turn0,
    turn1,
    send,
    cols,
    rq,
    rkv,
    keys,
    vals,
    ratt,
    done,
    x_ref,
    cot_ref,
    normed,
    win_t,
    wout,
    wout_t,
    dtok,
    dcot,
    sums,
    out_buf,
    part,
    pair,
    half_sum,
    got_chips,
    lined,
    row,
    got_tables,
    send_sem,
    cols_sem,
    send2_sem,
    recv2_sem,
    local_sem,
    sums_sem,
):
    me = lax.axis_index("cells") if remote else 0
    first_x = pltpu.make_async_copy(x_hbm.at[0:8], x_ref.at[0:8], local_sem.at[0])
    rest_x = pltpu.make_async_copy(x_hbm.at[8:LOCAL], x_ref.at[8:LOCAL], local_sem.at[1])
    all_cot = pltpu.make_async_copy(cot_hbm, cot_ref, local_sem.at[2])
    first_x.start()
    rest_x.start()
    all_cot.start()
    if remote:
        greet(("cells", "tables"))
    spread_weights(fw_ref, fwide, fproj_ref, fproj)
    ident = eye(FEATS)
    tok[:, 192:256] = jnp.zeros((FBLOCK * FEATS, 64), F32)
    lane = lax.broadcasted_iota(jnp.int32, (1, 128), 1)
    bias = jnp.where(lane < feat_count[0], 0.0, NEG).astype(F32)
    for ref, heads in ((vals0, range(4)), (vals1, range(4, 6))):
        ref[...] = jnp.zeros(ref.shape, BF16)
        for j in range(FBLOCK):
            for i, h in enumerate(heads):
                ref[j, 128 * i : 128 * i + FEATS, 128:256] = jnp.broadcast_to(ones_mask(h), (FEATS, 128))
    zero_pad = jnp.zeros((128 - FEATS, 128), BF16)

    def project(step):
        for j in range(FBLOCK):
            tok[pl.ds(FEATS * j, FEATS), 0:192] = mm(ident, x_ref[step * FBLOCK + j], NT)
        qkv[...] = mm(tok[...].astype(BF16), fwide[...])

    tiles_of_heads = ((range(4), vals0), (range(4, 6), vals1))

    def score_rows():
        scores = []
        for j in range(FBLOCK):
            rows = pl.ds(FEATS * j, FEATS)
            for tile, (heads, ref) in enumerate(tiles_of_heads):
                at = 128 * tile
                q = (qkv[rows, at : at + 128] * QSCALE).astype(BF16)
                k = qkv[rows, 256 + at : 384 + at].astype(BF16)
                v = qkv[rows, 512 + at : 640 + at].astype(BF16)
                pieces = []
                for i, h in enumerate(heads):
                    pieces += [k * head_mask(h), zero_pad]
                    ref[j, 128 * i : 128 * i + FEATS, 0:128] = v * head_mask(h)
                scores.append(mm(q, jnp.concatenate(pieces, axis=0), NT))
        return scores

    def attend(scores):
        for j in range(FBLOCK):
            rows = pl.ds(FEATS * j, FEATS)
            for tile, (heads, ref) in enumerate(tiles_of_heads):
                probs = []
                for i, h in enumerate(heads):
                    s = scores[2 * j + tile][:, 128 * i : 128 * i + 128] + bias
                    probs.append(jnp.exp2(s - jnp.max(s, axis=-1, keepdims=True)).astype(BF16))
                got = mm(jnp.concatenate(probs, axis=1), ref[j])
                att[rows, 128 * tile : 128 * tile + 128] = (got[:, :128] / got[:, 128:]).astype(BF16)

    def finish(step):
        mixed = mm(att[...], fproj[...])
        low, high = layer_norm(kept[:, 0:128] + mixed[:, 0:128], kept[:, 128:256] + mixed[:, 128:256])
        for j in range(FBLOCK):
            at = step * FBLOCK + j
            turn0[pl.ds(at, FEATS, stride=STRIDE), :] = low[FEATS * j : FEATS * j + FEATS]
            turn1[pl.ds(at, FEATS, stride=STRIDE), :] = high[FEATS * j : FEATS * j + FEATS]

    def blocks(step, _):
        scores = score_rows()
        finish(step - 2)
        kept[...] = tok[...]
        project(step)
        attend(scores)
        return 0

    def pack(p, group, half):
        def rows_of(ref, f):
            return ref[pl.ds(pl.multiple_of((p * OWN + f) * STRIDE + 16 * half, 8), 16), :]

        f = 2 * group
        at = 3 * group
        send[p, half, at] = rows_of(turn0, f).astype(BF16)
        high = rows_of(turn1, f)
        if f + 1 < OWN:
            at += 1
            send[p, half, at] = rows_of(turn0, f + 1).astype(BF16)
            high = high + pltpu.roll(rows_of(turn1, f + 1), 64, 1)
        send[p, half, at + 1] = high.astype(BF16)

    def pass_on(source, target, k, axis, p, send_s, recv_s):
        if not remote:
            pltpu.make_async_copy(source, target, recv_s).start()
            return

        @pl.when(k == 0)
        def _():
            pltpu.make_async_copy(source, target, recv_s).start()

        @pl.when(k != 0)
        def _():
            pltpu.make_async_remote_copy(
                src_ref=source,
                dst_ref=target,
                send_sem=send_s,
                recv_sem=recv_s,
                device_id={axis: p},
                device_id_type=MESH,
            ).start()

    def place(p):
        return me if remote else p

    first_x.wait()
    project(0)
    scores = score_rows()
    kept[...] = tok[...]
    project(1)
    attend(scores)
    rest_x.wait()
    lax.fori_loop(2, 2 + 16 // FBLOCK, blocks, 0)
    if remote:
        await_peers(("cells", "tables"))

    def first_half(k, _):
        p = lax.rem(me + k, PEERS)
        for group in range(4):
            pack(p, group, 0)
        pass_on(
            send.at[p, 0],
            cols.at[0, place(p)],
            k,
            "cells",
            p,
            send_sem,
            cols_sem.at[4],
        )
        return 0

    lax.fori_loop(0, PEERS, first_half, 0)
    lax.fori_loop(2 + 16 // FBLOCK, 32 // FBLOCK, blocks, 0)
    scores = score_rows()
    finish(32 // FBLOCK - 2)
    kept[...] = tok[...]
    attend(scores)
    finish(32 // FBLOCK - 1)
    for group in range(4):
        tiles = pl.ds(3 * group, min(3, TILES - 3 * group))

        def second_half(k, _):
            p = lax.rem(me + k, PEERS)
            pack(p, group, 1)
            pass_on(
                send.at[p, 1, tiles],
                cols.at[1, place(p), tiles],
                k,
                "cells",
                p,
                send_sem,
                cols_sem.at[group],
            )
            return 0

        lax.fori_loop(0, PEERS, second_half, 0)

    spread_weights(rw_ref, rwide, rproj_ref, rproj)
    lane = lax.broadcasted_iota(jnp.int32, (1, KEYS), 1)
    rbias = jnp.where(lane < train_count[0], 0.0, NEG).astype(F32)
    for h in range(HEADS):
        vals[KEYS * h : KEYS * h + KEYS, 128:256] = jnp.broadcast_to(ones_mask(h), (KEYS, 128))
    half_lane = lax.broadcasted_iota(jnp.int32, (1, 128), 1) < 64
    order_hidden(win_ref, wout_ref, win_t, wout, wout_t)
    sums[...] = jnp.zeros(sums.shape, F32)
    dtok[...] = jnp.zeros(dtok.shape, BF16)
    dcot[...] = jnp.zeros(dcot.shape, BF16)

    def column(f, _):
        @pl.when(f == 0)
        def _():
            ref = cols.at[0]
            pltpu.make_async_copy(ref, ref, cols_sem.at[4]).wait()

        for group in range(4):

            @pl.when(f == 2 * group)
            def _():
                ref = cols.at[1, :, pl.ds(3 * group, min(3, TILES - 3 * group))]
                pltpu.make_async_copy(ref, ref, cols_sem.at[group]).wait()

        odd = lax.rem(f, 2)
        at = 3 * (f // 2)

        def tokens(tile):
            return jnp.stack([cols[0, :, tile], cols[1, :, tile]], axis=1).reshape(ROWS, 128)

        low = tokens(at + odd)
        high = tokens(jnp.minimum(at + 2, TILES - 1)).astype(F32)
        high = jnp.where(half_lane, pltpu.roll(high, 64 * odd, 1), 0.0)
        x = jnp.concatenate([low, high.astype(BF16)], axis=1)
        rq[...] = (mm(x, rwide[:, 0:256]) * QSCALE).astype(BF16)
        rkv[...] = mm(x[0:KEYS], rwide[:, 256:768]).astype(BF16)
        for h in range(HEADS):
            at = 128 * (h // 4)
            rows = pl.ds(KEYS * h, KEYS)
            keys[rows, :] = rkv[:, at : at + 128] * head_mask(h)
            vals[rows, 0:128] = rkv[:, 256 + at : 384 + at] * head_mask(h)

        def score_pair(begin, first):
            at = 128 * (first // 4)
            return mm(rq[begin : begin + CHUNK, at : at + 128], keys[pl.ds(KEYS * first, 2 * KEYS), :], NT)

        def value_pair(first, score):
            probs = []
            for i in range(2):
                s = score[:, KEYS * i : KEYS * i + KEYS] + rbias
                probs.append(jnp.exp2(s - jnp.max(s, axis=-1, keepdims=True)).astype(BF16))
            return mm(jnp.concatenate(probs, axis=1), vals[pl.ds(KEYS * first, 2 * KEYS), :])

        units = [(begin, first) for begin in range(0, ROWS, CHUNK) for first in (0, 2, 4)]
        waiting = []
        got = None
        for n in range(len(units) + LAG):
            if n < len(units):
                waiting.append(score_pair(*units[n]))
            if n >= LAG:
                begin, first = units[n - LAG]
                more = value_pair(first, waiting.pop(0))
                got = more if first != 2 else got + more
                if first:
                    at = 128 * (first // 4)
                    ratt[begin : begin + CHUNK, at : at + 128] = (got[:, :128] / got[:, 128:]).astype(BF16)
        mixed = mm(ratt[...], rproj[...])
        low, high = layer_norm(low.astype(F32) + mixed[:, 0:128], high + mixed[:, 128:256])
        done[f, :, 0:32, :] = low.astype(BF16).reshape(PEERS, 32, 128)
        high = high.reshape(PEERS, 2, 16, 128)
        high = high[:, 0] + pltpu.roll(high[:, 1].reshape(PEERS * 16, 128), 64, 1).reshape(PEERS, 16, 128)
        done[f, :, 32:48, :] = high.astype(BF16)

        def to_peer(k, _):
            p = lax.rem(me + k, PEERS)
            pass_on(
                done.at[f, p],
                normed.at[f, place(p)],
                k,
                "cells",
                p,
                send2_sem,
                recv2_sem.at[f],
            )
            return 0

        return lax.fori_loop(0, PEERS, to_peer, 0)

    lax.fori_loop(0, OWN, column, 0)

    def unpack(f, _):
        pltpu.make_async_copy(normed.at[f], normed.at[f], recv2_sem.at[f]).wait()
        for p in range(PEERS):
            at = pl.multiple_of((p * OWN + f) * STRIDE, 8)
            turn0[pl.ds(at, LOCAL), :] = normed[f, p, 0:32, :].astype(F32)
            high = normed[f, p, 32:48, :].astype(F32)
            turn1[pl.ds(at, 16), :] = high
            turn1[pl.ds(at + 16, 16), :] = pltpu.roll(high, 64, 1)
        return 0

    all_cot.wait()
    lax.fori_loop(0, OWN, unpack, 0)

    def feed(step, _):
        feed_forward(step, cot_ref, turn0, turn1, win_t, wout, wout_t, dtok, dcot, sums, out_buf)
        rows = pl.ds(step * DROWS, DROWS)
        pltpu.make_async_copy(out_buf.at[rows], out_hbm.at[rows], local_sem.at[3]).start()
        return 0

    lax.fori_loop(0, LOCAL // DROWS, feed, 0)
    factor = 1.0 / math.sqrt(16 * ROWS * FEATS)
    part[0] = (sums[0, :, 0:128] * factor).astype(BF16)
    part[1] = (sums[1, :, 0:128] * (0.5 * factor)).astype(BF16)
    part[2, :, 0:64] = (sums[0, :, 128:192] * factor).astype(BF16)
    part[2, :, 64:128] = (sums[1, :, 128:192] * (0.5 * factor)).astype(BF16)

    table = lax.axis_index("tables") if remote else 0
    chip = me // 2
    core = me - 2 * chip
    theirs = pl.ds(pl.multiple_of((1 - core) * 384, 384), 384)
    mine = pl.ds(pl.multiple_of(core * 384, 384), 384)
    if remote:
        swap = pltpu.make_async_remote_copy(
            src_ref=part.at[:, theirs, :],
            dst_ref=pair,
            send_sem=sums_sem.at[0],
            recv_sem=sums_sem.at[1],
            device_id={"cells": 2 * chip + 1 - core},
            device_id_type=MESH,
        )
    else:
        swap = pltpu.make_async_copy(part.at[:, theirs, :], pair, sums_sem.at[1])
    swap.start()
    swap.wait()
    for t in range(3):
        half_sum[t] = (part[t, mine, :].astype(F32) + pair[t].astype(F32)).astype(BF16)

    def to_chip(k, _):
        p = lax.rem(chip + k, CHIPS)
        source = half_sum.at[:, pl.ds(pl.multiple_of(48 * p, 16), 48), :]
        target = got_chips.at[chip if remote else p]
        pass_on(source, target, k, "cells", 2 * p + core, sums_sem.at[2], sums_sem.at[3])
        return 0

    lax.fori_loop(0, CHIPS, to_chip, 0)
    lined[...] = jnp.zeros(lined.shape, F32)
    pltpu.make_async_copy(got_chips, got_chips, sums_sem.at[3]).wait()
    total = got_chips[0].astype(F32)
    for p in range(1, CHIPS):
        total = total + got_chips[p].astype(F32)
    for t in range(PEERS):
        for i in range(3):
            lined[t, 4 * i : 4 * i + 3, :] = total[i, 3 * t : 3 * t + 3, :]
    row[...] = lined[...].astype(BF16)

    def to_table(k, _):
        p = lax.rem(table + k, PEERS)
        pass_on(row.at[p], got_tables.at[table if remote else p], k, "tables", p, sums_sem.at[4], sums_sem.at[5])
        return 0

    lax.fori_loop(0, PEERS, to_table, 0)
    pltpu.make_async_copy(out_buf, out_hbm, local_sem.at[3]).wait()
    if remote:
        sent = send.at[pl.ds(0, PEERS - 1)]
        pltpu.make_async_copy(sent, sent, send_sem).wait()
        sent = normed.at[:, pl.ds(0, PEERS - 1)]
        pltpu.make_async_copy(sent, sent, send2_sem).wait()
        sent = got_chips.at[pl.ds(0, CHIPS - 1)]
        pltpu.make_async_copy(sent, sent, sums_sem.at[2]).wait()
        sent = got_tables.at[pl.ds(0, PEERS - 1)]
        pltpu.make_async_copy(sent, sent, sums_sem.at[4]).wait()
    pltpu.make_async_copy(got_tables, got_tables, sums_sem.at[5]).wait()
    final = got_tables[0].astype(F32)
    for t in range(1, PEERS):
        final = final + got_tables[t].astype(F32)
    grad_in_ref[:, 0:128] = final[0:3, :]
    grad_in_ref[:, 128:192] = final[8:11, 0:64]
    grad_out_ref[:, 0:128] = final[4:7, :]
    grad_out_ref[:, 128:192] = final[8:11, 64:128]


def whole_layer(
    x_t, feat_count, train_count, feat_qkv, feat_proj, row_qkv, row_proj, w_in, w_out_t, cot_t, remote=True
):
    vmem = pl.BlockSpec(memory_space=pltpu.VMEM)
    smem = pl.BlockSpec(memory_space=pltpu.SMEM)
    hbm = pl.BlockSpec(memory_space=pl.ANY)
    return pl.pallas_call(
        functools.partial(layer_kernel, remote),
        name="layer",
        out_shape=(
            jax.ShapeDtypeStruct((LOCAL, E, FEATS), BF16),
            jax.ShapeDtypeStruct((3, E), F32),
            jax.ShapeDtypeStruct((3, E), F32),
        ),
        in_specs=[smem, smem, hbm] + [vmem] * 6 + [hbm],
        out_specs=(hbm, vmem, vmem),
        scratch_shapes=[
            pltpu.VMEM((256, 768), BF16),
            pltpu.VMEM((256, 256), BF16),
            pltpu.VMEM((256, 768), BF16),
            pltpu.VMEM((256, 256), BF16),
            pltpu.VMEM((FBLOCK * FEATS, 256), F32),
            pltpu.VMEM((FBLOCK * FEATS, 256), F32),
            pltpu.VMEM((FBLOCK * FEATS, 768), F32),
            pltpu.VMEM((FBLOCK, 512, 256), BF16),
            pltpu.VMEM((FBLOCK, 256, 256), BF16),
            pltpu.VMEM((FBLOCK * FEATS, 256), BF16),
            pltpu.VMEM((FEATS * STRIDE, 128), F32),
            pltpu.VMEM((FEATS * STRIDE, 128), F32),
            pltpu.VMEM((PEERS, 2, TILES, 16, 128), BF16),
            pltpu.VMEM((2, PEERS, TILES, 16, 128), BF16),
            pltpu.VMEM((ROWS, 256), BF16),
            pltpu.VMEM((KEYS, 512), BF16),
            pltpu.VMEM((HEADS * KEYS, 128), BF16),
            pltpu.VMEM((HEADS * KEYS, 256), BF16),
            pltpu.VMEM((ROWS, 256), BF16),
            pltpu.VMEM((OWN, PEERS, 48, 128), BF16),
            pltpu.VMEM((LOCAL, E, FEATS), BF16),
            pltpu.VMEM((LOCAL, E, FEATS), BF16),
            pltpu.VMEM((OWN, PEERS, 48, 128), BF16),
            pltpu.VMEM((HID, E), BF16),
            pltpu.VMEM((HID, E), BF16),
            pltpu.VMEM((E, HID), BF16),
            pltpu.VMEM((DTOK, E), BF16),
            pltpu.VMEM((E, DTOK), BF16),
            pltpu.VMEM((2, HID, E), F32),
            pltpu.VMEM((LOCAL, E, FEATS), BF16),
            pltpu.VMEM((3, HID, 128), BF16),
            pltpu.VMEM((3, 384, 128), BF16),
            pltpu.VMEM((3, 384, 128), BF16),
            pltpu.VMEM((CHIPS, 3, 48, 128), BF16),
            pltpu.VMEM((PEERS, 16, 128), F32),
            pltpu.VMEM((PEERS, 16, 128), BF16),
            pltpu.VMEM((PEERS, 16, 128), BF16),
            pltpu.SemaphoreType.DMA,
            pltpu.SemaphoreType.DMA((5,)),
            pltpu.SemaphoreType.DMA,
            pltpu.SemaphoreType.DMA((OWN,)),
            pltpu.SemaphoreType.DMA((4,)),
            pltpu.SemaphoreType.DMA((6,)),
        ],
        compiler_params=pltpu.CompilerParams(
            collective_id=0 if remote else None, has_side_effects=True, vmem_limit_bytes=VMEM_LIMIT
        ),
    )(feat_count, train_count, x_t, feat_qkv, feat_proj, row_qkv, row_proj, w_in, w_out_t, cot_t)


def per_device(
    cells_in, train_count, feat_count, feat_qkv, feat_proj, row_qkv, row_proj, w_in, w_out, cotangent
):
    x_t = jnp.swapaxes(cells_in[0], 1, 2)
    cot_t = jnp.swapaxes(cotangent[0], 1, 2)
    out_t, grad_in, grad_out = whole_layer(
        x_t, feat_count, train_count, feat_qkv, feat_proj, row_qkv, row_proj, w_in, w_out.T, cot_t
    )
    return (jnp.swapaxes(out_t, 1, 2)[None], grad_in.T, grad_out)


def solution(mesh):
    return jax.shard_map(
        per_device,
        mesh=mesh,
        in_specs=(
            P("tables", "cells", None, None),
            P("tables"),
            P("tables"),
            P(),
            P(),
            P(),
            P(),
            P(),
            P(),
            P("tables", "cells", None, None),
        ),
        out_specs=(
            P("tables", "cells", None, None),
            P(None, ("tables", "cells")),
            P(("tables", "cells"), None),
        ),
        check_vma=False,
    )
```

time: 102 us -> 90.4 us (0.89)
  Pallas kernels: 97.3 us -> 84.5 us
  local copies, waits for them, and re-layouts: 2.25 us -> 3.85 us
    pallas_call x3 -> x1, Pallas kernels: 97.3 us -> 84.5 us  [whole_layer(): pl.pallas_call(functools.partial(layer_kernel, remote), name='layer', out...]
    unnamed x4 -> x7, local copies, waits for them, and re-layouts: 2.25 us -> 3.85 us
where the time goes in v3:
time: 90.4 us; the launch traced here: 90.3 us
  Pallas kernels  84.5 us (93%)
  local copies, waits for them, and re-layouts  3.85 us (4%)
  between operations  1.95 us (2%)
    pallas_call x1, Pallas kernels, whole_layer(): pl.pallas_call(functools.partial(layer_kernel, remote), name='layer', out...  84.5 us
    unnamed x7, local copies, waits for them, and re-layouts  3.85 us

profile of v3, /device:TPU:1, one launch (start us, length us, event | category | flops | bytes accessed | tf_op | source)
XLA Modules:
  0.0 90.3 jit_solution(2595904713993474509)
XLA Ops:
  1.9 84.5 %layer.1 = (bf16[32,192,112]{2,1,0:T(8,128)(2,1)}, f32[3,192]{1,0:T(4,128)}, f32[3,192]{1,0:T(4,128)}) custom-call(s32[1]{0:T(128)S(6)} %copy.17.feat_count, s32[1]{0:T(128)S(6)} %copy.16.train_count, bf16[32,192,112]{2,1,0:T(8,128)(2,1)} %bitcast.11, bf16[192,576]{1,0:T(8,128)(2,1)} %fw_ref.1, bf16[192,192]{1,0:T(8,128)(2,1)} %fproj_ref.1, ...), custom_call_target="tpu_custom_call" | custom-call | tf_op jit(solution)/shard_map/layer/pallas_call | solution.py:552
  86.4 0.0 copy-start.1
  86.4 0.0 copy-start
  86.4 2.7 %copy.18 = bf16[1,32,112,192]{2,3,1,0:T(8,128)(2,1)} copy(bf16[1,32,112,192]{2,3,1,0:T(8,128)(2,1)} %bitcast.13) | data formatting | bytes 2752512
  89.1 0.0 copy-done.1
  89.1 0.6 copy.19
  89.7 0.0 copy-done
  89.7 0.6 copy.20
Async XLA Ops:
  86.4 2.7 %copy-start.1 = (f32[3,192]{1,0:T(4,128)S(1)}, f32[3,192]{1,0:T(4,128)}, u32[]{:S(2)}) copy-start(f32[3,192]{1,0:T(4,128)} %get-tuple-element.7) | copy-start | bytes 6916
  86.4 3.3 %copy-start = (f32[3,192]{1,0:T(4,128)S(1)}, f32[3,192]{1,0:T(4,128)}, u32[]{:S(2)}) copy-start(f32[3,192]{1,0:T(4,128)} %get-tuple-element.14) | copy-start | bytes 6916

commit v4 on v3

--- a/solution.py
+++ b/solution.py
@@ -23,7 +23,7 @@
 BF16 = jnp.bfloat16
 NEG = -1e30
 QSCALE = math.log2(math.e) / math.sqrt(HEAD_DIM)
-VMEM_LIMIT = 60 * 1024 * 1024
+VMEM_LIMIT = 53 * 1024 * 1024
 MESH = pl.DeviceIdType.MESH
 
 NN = (((1,), (0,)), ((), ()))
@@ -90,6 +90,9 @@
 DROWS = 4
 DTOK = DROWS * 128
 HBLOCK = 256
+BLOCKS = 2
+AHEAD = 1
+STEPS = LOCAL // DROWS
 CHIPS = PEERS // 2
 
 
@@ -107,34 +110,40 @@
     wout_t[...] = (0.5 * mm(wout_ref[...], perm, NT)).astype(BF16)
 
 
-def feed_forward(step, cot_ref, turn0, turn1, win_t, wout, wout_t, tok, cot, sums, out_buf):
-    for j in range(DROWS):
-        at = step * DROWS + j
-        tok[128 * j : 128 * j + FEATS, 0:128] = turn0[pl.ds(at, FEATS, stride=STRIDE), :].astype(BF16)
-        tok[128 * j : 128 * j + FEATS, 128:192] = turn1[pl.ds(at, FEATS, stride=STRIDE), 0:64].astype(BF16)
-        cot[:, 128 * j : 128 * j + FEATS] = cot_ref[at]
-    x = tok[...]
-    c = cot[...]
-    total = mm(eye(E), x, NT)
+def feed_forward(first, cot_ref, turn0, turn1, win_t, wout, toks, acts, cot, sums):
+    units = []
+    for b in range(BLOCKS):
+        for j in range(DROWS):
+            at = (first + b) * DROWS + j
+            rows = pl.ds(128 * j, FEATS)
+            toks[first + b, rows, 0:128] = turn0[pl.ds(at, FEATS, stride=STRIDE), :].astype(BF16)
+            toks[first + b, rows, 128:192] = turn1[pl.ds(at, FEATS, stride=STRIDE), 0:64].astype(BF16)
+            cot[b, :, 128 * j : 128 * j + FEATS] = cot_ref[at]
+        units += [(b, begin) for begin in range(0, HID, HBLOCK)]
     waiting = []
-    for n in range(HID // HBLOCK + 1):
-        if n < HID // HBLOCK:
-            rows = pl.ds(HBLOCK * n, HBLOCK)
-            waiting.append((mm(win_t[rows, :], x, NT), mm(wout[rows, :], c)))
-        if n:
+    for n in range(len(units) + AHEAD):
+        if n < len(units):
+            b, begin = units[n]
+            rows = pl.ds(begin, HBLOCK)
+            waiting.append((mm(win_t[rows, :], toks[first + b], NT), mm(wout[rows, :], cot[b])))
+        if n >= AHEAD:
+            b, begin = units[n - AHEAD]
+            rows = pl.ds(begin, HBLOCK)
             pre, dact = waiting.pop(0)
-            begin = HBLOCK * (n - 1)
-            rows = pl.ds(begin, HBLOCK)
             u = pre * math.sqrt(0.5)
             twice = lax.erf(u) + 1.0
             act = (pre * twice).astype(BF16)
             slope = twice + u * jnp.exp2(math.log2(2.0 / math.sqrt(math.pi)) - (u * u) * math.log2(math.e))
             dpre = (dact * slope).astype(BF16)
-            sums[0, rows, :] += mm(dpre, x)
-            sums[1, rows, :] += mm(act, c, NT)
-            total = total + mm(wout_t[:, begin : begin + HBLOCK], act)
+            acts[first + b, rows, :] = act
+            sums[0, rows, :] += mm(dpre, toks[first + b])
+            sums[1, rows, :] += mm(act, cot[b], NT)
+
+
+def output_cells(step, wout_t, toks, acts, out_ref):
+    total = mm(eye(E), toks[step], NT) + mm(wout_t[...], acts[step])
     for j in range(DROWS):
-        out_buf[step * DROWS + j] = total[:, 128 * j : 128 * j + FEATS].astype(BF16)
+        out_ref[step * DROWS + j] = total[:, 128 * j : 128 * j + FEATS].astype(BF16)
 
 
 FBLOCK = 4
@@ -155,7 +164,7 @@
     win_ref,
     wout_ref,
     cot_hbm,
-    out_hbm,
+    out_ref,
     grad_in_ref,
     grad_out_ref,
     fwide,
@@ -184,10 +193,10 @@
     win_t,
     wout,
     wout_t,
-    dtok,
+    toks,
+    acts,
     dcot,
     sums,
-    out_buf,
     part,
     pair,
     half_sum,
@@ -370,7 +379,7 @@
     half_lane = lax.broadcasted_iota(jnp.int32, (1, 128), 1) < 64
     order_hidden(win_ref, wout_ref, win_t, wout, wout_t)
     sums[...] = jnp.zeros(sums.shape, F32)
-    dtok[...] = jnp.zeros(dtok.shape, BF16)
+    toks[...] = jnp.zeros(toks.shape, BF16)
     dcot[...] = jnp.zeros(dcot.shape, BF16)
 
     def column(f, _):
@@ -466,12 +475,15 @@
     lax.fori_loop(0, OWN, unpack, 0)
 
     def feed(step, _):
-        feed_forward(step, cot_ref, turn0, turn1, win_t, wout, wout_t, dtok, dcot, sums, out_buf)
-        rows = pl.ds(step * DROWS, DROWS)
-        pltpu.make_async_copy(out_buf.at[rows], out_hbm.at[rows], local_sem.at[3]).start()
+        feed_forward(BLOCKS * step, cot_ref, turn0, turn1, win_t, wout, toks, acts, dcot, sums)
         return 0
 
-    lax.fori_loop(0, LOCAL // DROWS, feed, 0)
+    lax.fori_loop(0, STEPS // BLOCKS, feed, 0)
+
+    def output(step, _):
+        output_cells(step, wout_t, toks, acts, out_ref)
+        return 0
+
     factor = 1.0 / math.sqrt(16 * ROWS * FEATS)
     part[0] = (sums[0, :, 0:128] * factor).astype(BF16)
     part[1] = (sums[1, :, 0:128] * (0.5 * factor)).astype(BF16)
@@ -495,6 +507,7 @@
     else:
         swap = pltpu.make_async_copy(part.at[:, theirs, :], pair, sums_sem.at[1])
     swap.start()
+    lax.fori_loop(0, STEPS // 8, output, 0)
     swap.wait()
     for t in range(3):
         half_sum[t] = (part[t, mine, :].astype(F32) + pair[t].astype(F32)).astype(BF16)
@@ -508,6 +521,7 @@
 
     lax.fori_loop(0, CHIPS, to_chip, 0)
     lined[...] = jnp.zeros(lined.shape, F32)
+    lax.fori_loop(STEPS // 8, STEPS * 5 // 8, output, 0)
     pltpu.make_async_copy(got_chips, got_chips, sums_sem.at[3]).wait()
     total = got_chips[0].astype(F32)
     for p in range(1, CHIPS):
@@ -523,7 +537,7 @@
         return 0
 
     lax.fori_loop(0, PEERS, to_table, 0)
-    pltpu.make_async_copy(out_buf, out_hbm, local_sem.at[3]).wait()
+    lax.fori_loop(STEPS * 5 // 8, STEPS, output, 0)
     if remote:
         sent = send.at[pl.ds(0, PEERS - 1)]
         pltpu.make_async_copy(sent, sent, send_sem).wait()
@@ -548,7 +562,7 @@
 ):
     vmem = pl.BlockSpec(memory_space=pltpu.VMEM)
     smem = pl.BlockSpec(memory_space=pltpu.SMEM)
-    hbm = pl.BlockSpec(memory_space=pl.ANY)
+    hbm = pl.BlockSpec(memory_space=pltpu.HBM)
     return pl.pallas_call(
         functools.partial(layer_kernel, remote),
         name="layer",
@@ -558,7 +572,7 @@
             jax.ShapeDtypeStruct((3, E), F32),
         ),
         in_specs=[smem, smem, hbm] + [vmem] * 6 + [hbm],
-        out_specs=(hbm, vmem, vmem),
+        out_specs=(vmem, vmem, vmem),
         scratch_shapes=[
             pltpu.VMEM((256, 768), BF16),
             pltpu.VMEM((256, 256), BF16),
@@ -586,10 +600,10 @@
             pltpu.VMEM((HID, E), BF16),
             pltpu.VMEM((HID, E), BF16),
             pltpu.VMEM((E, HID), BF16),
-            pltpu.VMEM((DTOK, E), BF16),
-            pltpu.VMEM((E, DTOK), BF16),
+            pltpu.VMEM((STEPS, DTOK, E), BF16),
+            pltpu.VMEM((STEPS, HID, DTOK), BF16),
+            pltpu.VMEM((BLOCKS, E, DTOK), BF16),
             pltpu.VMEM((2, HID, E), F32),
-            pltpu.VMEM((LOCAL, E, FEATS), BF16),
             pltpu.VMEM((3, HID, 128), BF16),
             pltpu.VMEM((3, 384, 128), BF16),
             pltpu.VMEM((3, 384, 128), BF16),
@@ -601,7 +615,7 @@
             pltpu.SemaphoreType.DMA((5,)),
             pltpu.SemaphoreType.DMA,
             pltpu.SemaphoreType.DMA((OWN,)),
-            pltpu.SemaphoreType.DMA((4,)),
+            pltpu.SemaphoreType.DMA((3,)),
             pltpu.SemaphoreType.DMA((6,)),
         ],
         compiler_params=pltpu.CompilerParams(

time: 90.4 us -> 92.4 us (1.022)
  local copies, waits for them, and re-layouts: 3.85 us -> 7.51 us
  Pallas kernels: 84.5 us -> 82.7 us
    unnamed x7 -> x11, local copies, waits for them, and re-layouts: 3.85 us -> 7.51 us
    pallas_call x1, Pallas kernels: 84.5 us -> 82.7 us  [whole_layer(): pl.pallas_call(functools.partial(layer_kernel, remote), name='layer', out...]
where the time goes in v4:
time: 92.4 us; the launch traced here: 92.1 us
  Pallas kernels  82.7 us (90%)
  local copies, waits for them, and re-layouts  7.51 us (8%)
  between operations  1.95 us (2%)
    pallas_call x1, Pallas kernels, whole_layer(): pl.pallas_call(functools.partial(layer_kernel, remote), name='layer', out...  82.7 us
    unnamed x11, local copies, waits for them, and re-layouts  7.51 us

profile of v4, /device:TPU:1, one launch (start us, length us, event | category | flops | bytes accessed | tf_op | source)
XLA Modules:
  0.0 92.1 jit_solution(6006094223833361857)
XLA Ops:
  1.9 0.0 copy-start
  1.9 0.9 %copy-done = bf16[192,576]{1,0:T(8,128)(2,1)S(1)} copy-done((bf16[192,576]{1,0:T(8,128)(2,1)S(1)}, bf16[192,576]{1,0:T(8,128)(2,1)}, u32[]{:S(2)}) %copy-start) | copy-done | bytes 221208
  2.9 0.0 copy-start.1
  2.9 0.9 %copy-done.1 = bf16[192,576]{1,0:T(8,128)(2,1)S(1)} copy-done((bf16[192,576]{1,0:T(8,128)(2,1)S(1)}, bf16[192,576]{1,0:T(8,128)(2,1)}, u32[]{:S(2)}) %copy-start.1) | copy-done | bytes 221208
  3.8 0.0 copy-start.2
  3.8 0.9 copy-done.2
  4.7 0.0 copy-start.3
  4.7 0.9 copy-done.3
  5.6 82.7 %layer.1 = (bf16[32,192,112]{2,1,0:T(8,128)(2,1)}, f32[3,192]{1,0:T(4,128)S(1)}, f32[3,192]{1,0:T(4,128)S(1)}) custom-call(s32[1]{0:T(128)S(6)} %copy.17.feat_count, s32[1]{0:T(128)S(6)} %copy.16.train_count, bf16[32,192,112]{2,1,0:T(8,128)(2,1)} %bitcast.12, bf16[192,576]{1,0:T(8,128)(2,1)S(1)} %copy-done, bf16[192,192]{1,0:T(8,128)(2,1)S(1)} %copy-done.2, ...), custom_call_target="tpu_custom_call" | custom-call | tf_op jit(solution)/shard_map/layer/pallas_call | solution.py:566
  88.3 2.7 %copy.18 = bf16[1,32,112,192]{2,3,1,0:T(8,128)(2,1)} copy(bf16[1,32,112,192]{2,3,1,0:T(8,128)(2,1)} %bitcast.14) | data formatting | bytes 2752512
  91.0 0.6 copy.19
  91.5 0.6 copy.20
Async XLA Ops:
  1.9 0.9 %copy-start = (bf16[192,576]{1,0:T(8,128)(2,1)S(1)}, bf16[192,576]{1,0:T(8,128)(2,1)}, u32[]{:S(2)}) copy-start(bf16[192,576]{1,0:T(8,128)(2,1)} %fw_ref.1) | copy-start | bytes 663556
  2.9 0.9 %copy-start.1 = (bf16[192,576]{1,0:T(8,128)(2,1)S(1)}, bf16[192,576]{1,0:T(8,128)(2,1)}, u32[]{:S(2)}) copy-start(bf16[192,576]{1,0:T(8,128)(2,1)} %rw_ref.1) | copy-start | bytes 663556
  3.8 0.9 copy-start.2
  4.7 0.9 copy-start.3

commit v5 on v4

--- a/solution.py
+++ b/solution.py
@@ -23,7 +23,7 @@
 BF16 = jnp.bfloat16
 NEG = -1e30
 QSCALE = math.log2(math.e) / math.sqrt(HEAD_DIM)
-VMEM_LIMIT = 53 * 1024 * 1024
+VMEM_LIMIT = 60 * 1024 * 1024
 MESH = pl.DeviceIdType.MESH
 
 NN = (((1,), (0,)), ((), ()))
@@ -150,6 +150,7 @@
 TILES = 11
 CHUNK = 256
 LAG = 2
+FILL = 2
 
 
 def layer_kernel(
@@ -157,14 +158,14 @@
     feat_count,
     train_count,
     x_hbm,
-    fw_ref,
-    fproj_ref,
-    rw_ref,
-    rproj_ref,
-    win_ref,
-    wout_ref,
+    fw_hbm,
+    fproj_hbm,
+    rw_hbm,
+    rproj_hbm,
+    win_hbm,
+    wout_hbm,
     cot_hbm,
-    out_ref,
+    out_hbm,
     grad_in_ref,
     grad_out_ref,
     fwide,
@@ -182,11 +183,16 @@
     send,
     cols,
     rq,
-    rkv,
     keys,
     vals,
     ratt,
     done,
+    fw_ref,
+    fproj_ref,
+    rw_ref,
+    rproj_ref,
+    win_ref,
+    wout_ref,
     x_ref,
     cot_ref,
     normed,
@@ -197,6 +203,7 @@
     acts,
     dcot,
     sums,
+    out_buf,
     part,
     pair,
     half_sum,
@@ -215,11 +222,26 @@
     first_x = pltpu.make_async_copy(x_hbm.at[0:8], x_ref.at[0:8], local_sem.at[0])
     rest_x = pltpu.make_async_copy(x_hbm.at[8:LOCAL], x_ref.at[8:LOCAL], local_sem.at[1])
     all_cot = pltpu.make_async_copy(cot_hbm, cot_ref, local_sem.at[2])
+    pairs = (
+        (fw_hbm, fw_ref),
+        (fproj_hbm, fproj_ref),
+        (rw_hbm, rw_ref),
+        (rproj_hbm, rproj_ref),
+        (win_hbm, win_ref),
+        (wout_hbm, wout_ref),
+    )
+    weights = [pltpu.make_async_copy(a, b, local_sem.at[4 + i]) for i, (a, b) in enumerate(pairs)]
+    weights[0].start()
+    weights[1].start()
     first_x.start()
     rest_x.start()
+    for copy in weights[2:]:
+        copy.start()
     all_cot.start()
     if remote:
         greet(("cells", "tables"))
+    weights[0].wait()
+    weights[1].wait()
     spread_weights(fw_ref, fwide, fproj_ref, fproj)
     ident = eye(FEATS)
     tok[:, 192:256] = jnp.zeros((FBLOCK * FEATS, 64), F32)
@@ -371,23 +393,21 @@
 
         lax.fori_loop(0, PEERS, second_half, 0)
 
+    for copy in weights[2:]:
+        copy.wait()
     spread_weights(rw_ref, rwide, rproj_ref, rproj)
     lane = lax.broadcasted_iota(jnp.int32, (1, KEYS), 1)
     rbias = jnp.where(lane < train_count[0], 0.0, NEG).astype(F32)
     for h in range(HEADS):
-        vals[KEYS * h : KEYS * h + KEYS, 128:256] = jnp.broadcast_to(ones_mask(h), (KEYS, 128))
+        for odd in range(2):
+            vals[odd, KEYS * h : KEYS * h + KEYS, 128:256] = jnp.broadcast_to(ones_mask(h), (KEYS, 128))
     half_lane = lax.broadcasted_iota(jnp.int32, (1, 128), 1) < 64
     order_hidden(win_ref, wout_ref, win_t, wout, wout_t)
     sums[...] = jnp.zeros(sums.shape, F32)
     toks[...] = jnp.zeros(toks.shape, BF16)
     dcot[...] = jnp.zeros(dcot.shape, BF16)
 
-    def column(f, _):
-        @pl.when(f == 0)
-        def _():
-            ref = cols.at[0]
-            pltpu.make_async_copy(ref, ref, cols_sem.at[4]).wait()
-
+    def arrive(f):
         for group in range(4):
 
             @pl.when(f == 2 * group)
@@ -395,7 +415,7 @@
                 ref = cols.at[1, :, pl.ds(3 * group, min(3, TILES - 3 * group))]
                 pltpu.make_async_copy(ref, ref, cols_sem.at[group]).wait()
 
-        odd = lax.rem(f, 2)
+    def column_of(f, odd):
         at = 3 * (f // 2)
 
         def tokens(tile):
@@ -403,63 +423,95 @@
 
         low = tokens(at + odd)
         high = tokens(jnp.minimum(at + 2, TILES - 1)).astype(F32)
-        high = jnp.where(half_lane, pltpu.roll(high, 64 * odd, 1), 0.0)
+        if odd:
+            high = pltpu.roll(high, 64, 1)
+        return low, jnp.where(half_lane, high, 0.0)
+
+    def prepare(f, odd):
+        low, high = column_of(f, odd)
         x = jnp.concatenate([low, high.astype(BF16)], axis=1)
-        rq[...] = (mm(x, rwide[:, 0:256]) * QSCALE).astype(BF16)
-        rkv[...] = mm(x[0:KEYS], rwide[:, 256:768]).astype(BF16)
+        rq[odd] = (mm(x, rwide[:, 0:256]) * QSCALE).astype(BF16)
+        rkv = mm(x[0:KEYS], rwide[:, 256:768]).astype(BF16)
         for h in range(HEADS):
             at = 128 * (h // 4)
             rows = pl.ds(KEYS * h, KEYS)
-            keys[rows, :] = rkv[:, at : at + 128] * head_mask(h)
-            vals[rows, 0:128] = rkv[:, 256 + at : 384 + at] * head_mask(h)
-
-        def score_pair(begin, first):
-            at = 128 * (first // 4)
-            return mm(rq[begin : begin + CHUNK, at : at + 128], keys[pl.ds(KEYS * first, 2 * KEYS), :], NT)
-
-        def value_pair(first, score):
-            probs = []
-            for i in range(2):
-                s = score[:, KEYS * i : KEYS * i + KEYS] + rbias
-                probs.append(jnp.exp2(s - jnp.max(s, axis=-1, keepdims=True)).astype(BF16))
-            return mm(jnp.concatenate(probs, axis=1), vals[pl.ds(KEYS * first, 2 * KEYS), :])
-
-        units = [(begin, first) for begin in range(0, ROWS, CHUNK) for first in (0, 2, 4)]
+            keys[odd, rows, :] = rkv[:, at : at + 128] * head_mask(h)
+            vals[odd, rows, 0:128] = rkv[:, 256 + at : 384 + at] * head_mask(h)
+
+    units = [(begin, first) for begin in range(0, ROWS, CHUNK) for first in (0, 2, 4)]
+
+    def score_pair(odd, begin, first):
+        at = 128 * (first // 4)
+        return mm(rq[odd, begin : begin + CHUNK, at : at + 128], keys[odd, pl.ds(KEYS * first, 2 * KEYS), :], NT)
+
+    def value_pair(odd, first, score):
+        probs = []
+        for i in range(2):
+            s = score[:, KEYS * i : KEYS * i + KEYS] + rbias
+            probs.append(jnp.exp2(s - jnp.max(s, axis=-1, keepdims=True)).astype(BF16))
+        return mm(jnp.concatenate(probs, axis=1), vals[odd, pl.ds(KEYS * first, 2 * KEYS), :])
+
+    def attend_rows(odd, fill=None):
         waiting = []
         got = None
         for n in range(len(units) + LAG):
             if n < len(units):
-                waiting.append(score_pair(*units[n]))
+                waiting.append(score_pair(odd, *units[n]))
+            if n == FILL and fill is not None:
+                fill()
             if n >= LAG:
                 begin, first = units[n - LAG]
-                more = value_pair(first, waiting.pop(0))
+                more = value_pair(odd, first, waiting.pop(0))
                 got = more if first != 2 else got + more
                 if first:
                     at = 128 * (first // 4)
-                    ratt[begin : begin + CHUNK, at : at + 128] = (got[:, :128] / got[:, 128:]).astype(BF16)
-        mixed = mm(ratt[...], rproj[...])
+                    ratt[odd, begin : begin + CHUNK, at : at + 128] = (got[:, :128] / got[:, 128:]).astype(BF16)
+
+    def finish_column(f, odd):
+        low, high = column_of(f, odd)
+        mixed = mm(ratt[odd], rproj[...])
         low, high = layer_norm(low.astype(F32) + mixed[:, 0:128], high + mixed[:, 128:256])
         done[f, :, 0:32, :] = low.astype(BF16).reshape(PEERS, 32, 128)
         high = high.reshape(PEERS, 2, 16, 128)
         high = high[:, 0] + pltpu.roll(high[:, 1].reshape(PEERS * 16, 128), 64, 1).reshape(PEERS, 16, 128)
         done[f, :, 32:48, :] = high.astype(BF16)
 
+    def send_column(f):
         def to_peer(k, _):
             p = lax.rem(me + k, PEERS)
-            pass_on(
-                done.at[f, p],
-                normed.at[f, place(p)],
-                k,
-                "cells",
-                p,
-                send2_sem,
-                recv2_sem.at[f],
-            )
+            pass_on(done.at[f, p], normed.at[f, place(p)], k, "cells", p, send2_sem, recv2_sem.at[f])
             return 0
 
-        return lax.fori_loop(0, PEERS, to_peer, 0)
-
-    lax.fori_loop(0, OWN, column, 0)
+        lax.fori_loop(0, PEERS, to_peer, 0)
+
+    pltpu.make_async_copy(cols.at[0], cols.at[0], cols_sem.at[4]).wait()
+    arrive(0)
+    prepare(0, 0)
+    attend_rows(0, lambda: prepare(1, 1))
+
+    def two_columns(g, _):
+        f = 2 * g
+        arrive(f)
+
+        def fill():
+            finish_column(f - 2, 0)
+            prepare(f, 0)
+
+        attend_rows(1, fill)
+        send_column(f - 2)
+
+        def fill_next():
+            finish_column(f - 1, 1)
+
+            prepare(jnp.minimum(f + 1, OWN - 2), 1)
+
+        attend_rows(0, fill_next)
+        send_column(f - 1)
+        return 0
+
+    lax.fori_loop(1, 4, two_columns, 0)
+    finish_column(OWN - 1, 0)
+    send_column(OWN - 1)
 
     def unpack(f, _):
         pltpu.make_async_copy(normed.at[f], normed.at[f], recv2_sem.at[f]).wait()
@@ -481,7 +533,9 @@
     lax.fori_loop(0, STEPS // BLOCKS, feed, 0)
 
     def output(step, _):
-        output_cells(step, wout_t, toks, acts, out_ref)
+        output_cells(step, wout_t, toks, acts, out_buf)
+        rows = pl.ds(step * DROWS, DROWS)
+        pltpu.make_async_copy(out_buf.at[rows], out_hbm.at[rows], local_sem.at[3]).start()
         return 0
 
     factor = 1.0 / math.sqrt(16 * ROWS * FEATS)
@@ -547,6 +601,7 @@
         pltpu.make_async_copy(sent, sent, sums_sem.at[2]).wait()
         sent = got_tables.at[pl.ds(0, PEERS - 1)]
         pltpu.make_async_copy(sent, sent, sums_sem.at[4]).wait()
+    pltpu.make_async_copy(out_buf, out_hbm, local_sem.at[3]).wait()
     pltpu.make_async_copy(got_tables, got_tables, sums_sem.at[5]).wait()
     final = got_tables[0].astype(F32)
     for t in range(1, PEERS):
@@ -562,7 +617,7 @@
 ):
     vmem = pl.BlockSpec(memory_space=pltpu.VMEM)
     smem = pl.BlockSpec(memory_space=pltpu.SMEM)
-    hbm = pl.BlockSpec(memory_space=pltpu.HBM)
+    hbm = pl.BlockSpec(memory_space=pl.ANY)
     return pl.pallas_call(
         functools.partial(layer_kernel, remote),
         name="layer",
@@ -571,8 +626,8 @@
             jax.ShapeDtypeStruct((3, E), F32),
             jax.ShapeDtypeStruct((3, E), F32),
         ),
-        in_specs=[smem, smem, hbm] + [vmem] * 6 + [hbm],
-        out_specs=(vmem, vmem, vmem),
+        in_specs=[smem, smem] + [hbm] * 8,
+        out_specs=(hbm, vmem, vmem),
         scratch_shapes=[
             pltpu.VMEM((256, 768), BF16),
             pltpu.VMEM((256, 256), BF16),
@@ -588,12 +643,17 @@
             pltpu.VMEM((FEATS * STRIDE, 128), F32),
             pltpu.VMEM((PEERS, 2, TILES, 16, 128), BF16),
             pltpu.VMEM((2, PEERS, TILES, 16, 128), BF16),
-            pltpu.VMEM((ROWS, 256), BF16),
-            pltpu.VMEM((KEYS, 512), BF16),
-            pltpu.VMEM((HEADS * KEYS, 128), BF16),
-            pltpu.VMEM((HEADS * KEYS, 256), BF16),
-            pltpu.VMEM((ROWS, 256), BF16),
+            pltpu.VMEM((2, ROWS, 256), BF16),
+            pltpu.VMEM((2, HEADS * KEYS, 128), BF16),
+            pltpu.VMEM((2, HEADS * KEYS, 256), BF16),
+            pltpu.VMEM((2, ROWS, 256), BF16),
             pltpu.VMEM((OWN, PEERS, 48, 128), BF16),
+            pltpu.VMEM((E, 3 * E), BF16),
+            pltpu.VMEM((E, E), BF16),
+            pltpu.VMEM((E, 3 * E), BF16),
+            pltpu.VMEM((E, E), BF16),
+            pltpu.VMEM((E, HID), BF16),
+            pltpu.VMEM((E, HID), BF16),
             pltpu.VMEM((LOCAL, E, FEATS), BF16),
             pltpu.VMEM((LOCAL, E, FEATS), BF16),
             pltpu.VMEM((OWN, PEERS, 48, 128), BF16),
@@ -604,6 +664,7 @@
             pltpu.VMEM((STEPS, HID, DTOK), BF16),
             pltpu.VMEM((BLOCKS, E, DTOK), BF16),
             pltpu.VMEM((2, HID, E), F32),
+            pltpu.VMEM((LOCAL, E, FEATS), BF16),
             pltpu.VMEM((3, HID, 128), BF16),
             pltpu.VMEM((3, 384, 128), BF16),
             pltpu.VMEM((3, 384, 128), BF16),
@@ -615,13 +676,46 @@
             pltpu.SemaphoreType.DMA((5,)),
             pltpu.SemaphoreType.DMA,
             pltpu.SemaphoreType.DMA((OWN,)),
-            pltpu.SemaphoreType.DMA((3,)),
+            pltpu.SemaphoreType.DMA((10,)),
             pltpu.SemaphoreType.DMA((6,)),
         ],
         compiler_params=pltpu.CompilerParams(
             collective_id=0 if remote else None, has_side_effects=True, vmem_limit_bytes=VMEM_LIMIT
         ),
     )(feat_count, train_count, x_t, feat_qkv, feat_proj, row_qkv, row_proj, w_in, w_out_t, cot_t)
+
+
+PIECES = 8
+
+
+def closing_kernel(cells_hbm, a_hbm, b_hbm, cells_out, a_out, b_out, cells, a, b, in_sem, out_sem):
+    small = ((a_hbm, a, a_out), (b_hbm, b, b_out))
+    size = LOCAL // PIECES
+    steps = [(source, hold, target) for source, hold, target in small]
+    steps += [tuple(ref.at[pl.ds(size * i, size)] for ref in (cells_hbm, cells, cells_out)) for i in range(PIECES)]
+    loads = [pltpu.make_async_copy(source, hold, in_sem.at[i]) for i, (source, hold, _) in enumerate(steps)]
+    stores = [pltpu.make_async_copy(hold, target, out_sem.at[i]) for i, (_, hold, target) in enumerate(steps)]
+    for copy in loads:
+        copy.start()
+    for load, store in zip(loads, stores):
+        load.wait()
+        store.start()
+    for copy in stores:
+        copy.wait()
+
+
+def close(cells, a, b):
+    hbm = pl.BlockSpec(memory_space=pl.ANY)
+    return pl.pallas_call(
+        closing_kernel,
+        name="closing_copies",
+        out_shape=tuple(jax.ShapeDtypeStruct(v.shape, v.dtype) for v in (cells, a, b)),
+        in_specs=[hbm] * 3,
+        out_specs=(hbm,) * 3,
+        scratch_shapes=[pltpu.VMEM(v.shape, v.dtype) for v in (cells, a, b)]
+        + [pltpu.SemaphoreType.DMA((PIECES + 2,)), pltpu.SemaphoreType.DMA((PIECES + 2,))],
+        compiler_params=pltpu.CompilerParams(vmem_limit_bytes=VMEM_LIMIT),
+    )(cells, a, b)
 
 
 def per_device(
@@ -632,6 +726,7 @@
     out_t, grad_in, grad_out = whole_layer(
         x_t, feat_count, train_count, feat_qkv, feat_proj, row_qkv, row_proj, w_in, w_out.T, cot_t
     )
+    out_t, grad_in, grad_out = close(out_t, grad_in, grad_out)
     return (jnp.swapaxes(out_t, 1, 2)[None], grad_in.T, grad_out)
 
 

time: 92.4 us -> 85.9 us (0.930)
  local copies, waits for them, and re-layouts: 7.51 us -> 0 us
    unnamed x11 -> x0, local copies, waits for them, and re-layouts: 7.51 us -> none
    pallas_call x0 -> x1, Pallas kernels: none -> 2.34 us  [close(): pl.pallas_call(closing_kernel, name='closing_copies', out_shape=tuple((ja...]
    pallas_call x1, Pallas kernels: 82.7 us -> 81.3 us  [whole_layer(): pl.pallas_call(functools.partial(layer_kernel, remote), name='layer', out...]
where the time goes in v5:
time: 85.9 us; the launch traced here: 85.7 us
  Pallas kernels  83.6 us (97%)
  between operations  2.09 us (2%)
    pallas_call x1, Pallas kernels, whole_layer(): pl.pallas_call(functools.partial(layer_kernel, remote), name='layer', out...  81.3 us
    pallas_call x1, Pallas kernels, close(): pl.pallas_call(closing_kernel, name='closing_copies', out_shape=tuple((ja...  2.34 us

profile of v5, /device:TPU:1, one launch (start us, length us, event | category | flops | bytes accessed | tf_op | source)
XLA Modules:
  0.0 85.7 jit_solution(16036834798396042556)
XLA Ops:
  1.9 81.3 %layer.1 = (bf16[32,192,112]{2,1,0:T(8,128)(2,1)}, f32[3,192]{1,0:T(4,128)}, f32[3,192]{1,0:T(4,128)}) custom-call(s32[1]{0:T(128)S(6)} %copy.14.feat_count, s32[1]{0:T(128)S(6)} %copy.13.train_count, bf16[32,192,112]{2,1,0:T(8,128)(2,1)} %bitcast.11, bf16[192,576]{1,0:T(8,128)(2,1)} %fw_hbm.1, bf16[192,192]{1,0:T(8,128)(2,1)} %fproj_hbm.1, ...), custom_call_target="tpu_custom_call" | custom-call | tf_op jit(solution)/shard_map/layer/pallas_call | solution.py:621
  83.2 2.3 %closing_copies.1 = (bf16[32,192,112]{2,1,0:T(8,128)(2,1)}, f32[3,192]{1,0:T(4,128)}, f32[3,192]{1,0:T(4,128)}) custom-call(bf16[32,192,112]{2,1,0:T(8,128)(2,1)} %get-tuple-element.9.cells_hbm, f32[3,192]{1,0:T(4,128)} %get-tuple-element.10.a_hbm, f32[3,192]{1,0:T(4,128)} %get-tuple-element.11.b_hbm), custom_call_target="tpu_custom_call" | custom-call | tf_op jit(solution)/shard_map/closing_copies/pallas_call | solution.py:709

commit v6 on v5

--- a/solution.py
+++ b/solution.py
@@ -91,7 +91,7 @@
 DTOK = DROWS * 128
 HBLOCK = 256
 BLOCKS = 2
-AHEAD = 1
+AHEAD = 2
 STEPS = LOCAL // DROWS
 CHIPS = PEERS // 2
 

time: 85.9 us -> 85.1 us (level)
  no operation moved by 1% of the time
where the time goes in v6:
time: 85.1 us; the launch traced here: 85 us
  Pallas kernels  82.9 us (97%)
  between operations  2.09 us (2%)
    pallas_call x1, Pallas kernels, whole_layer(): pl.pallas_call(functools.partial(layer_kernel, remote), name='layer', out...  80.5 us
    pallas_call x1, Pallas kernels, close(): pl.pallas_call(closing_kernel, name='closing_copies', out_shape=tuple((ja...  2.34 us

profile of v6, /device:TPU:1, one launch (start us, length us, event | category | flops | bytes accessed | tf_op | source)
XLA Modules:
  0.0 85.0 jit_solution(16341104182978084288)
XLA Ops:
  1.9 80.5 %layer.1 = (bf16[32,192,112]{2,1,0:T(8,128)(2,1)}, f32[3,192]{1,0:T(4,128)}, f32[3,192]{1,0:T(4,128)}) custom-call(s32[1]{0:T(128)S(6)} %copy.14.feat_count, s32[1]{0:T(128)S(6)} %copy.13.train_count, bf16[32,192,112]{2,1,0:T(8,128)(2,1)} %bitcast.11, bf16[192,576]{1,0:T(8,128)(2,1)} %fw_hbm.1, bf16[192,192]{1,0:T(8,128)(2,1)} %fproj_hbm.1, ...), custom_call_target="tpu_custom_call" | custom-call | tf_op jit(solution)/shard_map/layer/pallas_call | solution.py:621
  82.5 2.3 %closing_copies.1 = (bf16[32,192,112]{2,1,0:T(8,128)(2,1)}, f32[3,192]{1,0:T(4,128)}, f32[3,192]{1,0:T(4,128)}) custom-call(bf16[32,192,112]{2,1,0:T(8,128)(2,1)} %get-tuple-element.9.cells_hbm, f32[3,192]{1,0:T(4,128)} %get-tuple-element.10.a_hbm, f32[3,192]{1,0:T(4,128)} %get-tuple-element.11.b_hbm), custom_call_target="tpu_custom_call" | custom-call | tf_op jit(solution)/shard_map/closing_copies/pallas_call | solution.py:709
